TPU v7x, 8 devices: a whole 2x2x1 slice. The times are simulated.
8 devices in a mesh: data: 1 (over z), stage: 8 (over y, x, core).
Axes of the slice: x: 2, y: 2, z: 1, core: 2. Of those that a mesh axis runs over, the one named last changes fastest.
Arguments:
- x: bfloat16 [1, 512, 1280], P('data')
- y: bfloat16 [1, 512, 1280], P('data')
- w_qkv: bfloat16 [8, 1280, 3840], P('stage')
- w_out: bfloat16 [8, 1280, 1280], P('stage')
- w_up: bfloat16 [8, 1280, 5120], P('stage')
- w_down: bfloat16 [8, 5120, 1280], P('stage')
- norm_gain: bfloat16 [8, 2, 1280], P('stage')
Outputs:
- output 1: float32 [1], P('data')
- output 2: float32 [8, 1280, 3840], P(('data', 'stage'))
- output 3: float32 [8, 1280, 1280], P(('data', 'stage'))
- output 4: float32 [8, 1280, 5120], P(('data', 'stage'))
- output 5: float32 [8, 5120, 1280], P(('data', 'stage'))
- output 6: float32 [8, 2, 1280], P(('data', 'stage'))
All inputs are finite; a program needn't handle non-finite values.
Results may differ from a plain program's by a relative error of at most 0.0141127.
Values are sent between devices in bfloat16 or wider.
A program may use at most 1 GiB of HBM per device.

v0:
```python
import jax
import jax.numpy as jnp
from jax import lax
from jax.sharding import PartitionSpec as P

HEAD_DIM = 64
PIECE_LEN = 256
EPS = 1e-6


def rms_norm(hidden, gain):
    hid_f = hidden.astype(jnp.float32)
    inv_rms = lax.rsqrt(jnp.mean(hid_f * hid_f, axis=-1, keepdims=True) + EPS)
    return (hid_f * inv_rms * gain.astype(jnp.float32)).astype(jnp.bfloat16)


def attend(qkv_rows, keys_full, values_full, row_start):
    q_len = qkv_rows.shape[0]
    seq_len = keys_full.shape[0]
    width = keys_full.shape[1]
    num_heads = width // HEAD_DIM
    queries = qkv_rows[:, :width].reshape(q_len, num_heads, HEAD_DIM)
    keys_h = keys_full.reshape(seq_len, num_heads, HEAD_DIM)
    values_h = values_full.reshape(seq_len, num_heads, HEAD_DIM)
    scores = jnp.einsum('qhd,khd->hqk', queries, keys_h, preferred_element_type=jnp.float32) * HEAD_DIM ** -0.5
    query_pos = row_start + jnp.arange(q_len)
    causal_mask = jnp.arange(seq_len)[None, :] <= query_pos[:, None]
    scores = jnp.where(causal_mask[None], scores, -1e30)
    probs_bf = jax.nn.softmax(scores, axis=-1).astype(jnp.bfloat16)
    att_out = jnp.einsum('hqk,khd->qhd', probs_bf, values_h, preferred_element_type=jnp.float32)
    return att_out.astype(jnp.bfloat16).reshape(q_len, width)


def stage_piece(hidden, params, k_cache, v_cache, row_start):
    w_qkv, w_out, w_up, w_down, norm_gain = params
    width = hidden.shape[1]
    new_keys = []
    new_values = []
    for layer_idx in range(w_qkv.shape[0]):
        normed = rms_norm(hidden, norm_gain[layer_idx, 0])
        qkv_rows = jnp.dot(normed, w_qkv[layer_idx], preferred_element_type=jnp.float32).astype(jnp.bfloat16)
        key_rows = qkv_rows[:, width:2 * width]
        value_rows = qkv_rows[:, 2 * width:]
        keys_full = lax.dynamic_update_slice(k_cache[layer_idx], key_rows, (row_start, 0))
        values_full = lax.dynamic_update_slice(v_cache[layer_idx], value_rows, (row_start, 0))
        att_mix = attend(qkv_rows, keys_full, values_full, row_start)
        hidden = (hidden.astype(jnp.float32) + jnp.dot(att_mix, w_out[layer_idx], preferred_element_type=jnp.float32)).astype(jnp.bfloat16)
        normed = rms_norm(hidden, norm_gain[layer_idx, 1])
        upper = jnp.dot(normed, w_up[layer_idx], preferred_element_type=jnp.float32)
        act_bf = jax.nn.gelu(upper).astype(jnp.bfloat16)
        hidden = (hidden.astype(jnp.float32) + jnp.dot(act_bf, w_down[layer_idx], preferred_element_type=jnp.float32)).astype(jnp.bfloat16)
        new_keys.append(key_rows)
        new_values.append(value_rows)
    return hidden, jnp.stack(new_keys), jnp.stack(new_values)


def solution(mesh):
    stages = mesh.shape['stage']
    fwd_pairs = [(src, src + 1) for src in range(stages - 1)]
    bwd_pairs = [(src + 1, src) for src in range(stages - 1)]

    def per_device(x, y, w_qkv, w_out, w_up, w_down, norm_gain):
        params = (w_qkv, w_out, w_up, w_down, norm_gain)
        stage_idx = lax.axis_index('stage')
        is_last = stage_idx == stages - 1
        seq_len = x.shape[1]
        width = x.shape[2]
        layers = w_qkv.shape[0]
        pieces = seq_len // PIECE_LEN
        ticks = pieces + stages - 1
        norm_count = float(seq_len * width)
        x_pieces = x[0].reshape(pieces, PIECE_LEN, width)
        y_pieces = y[0].reshape(pieces, PIECE_LEN, width)
        act_shape = (PIECE_LEN, width)

        def fwd_tick(carry, tick_idx):
            recv, k_cache, v_cache, saved_in, top_grad, loss_acc = carry
            piece_idx = tick_idx - stage_idx
            active = (piece_idx >= 0) & (piece_idx < pieces)
            piece_pos = jnp.clip(piece_idx, 0, pieces - 1)
            row_start = piece_pos * PIECE_LEN
            first_rows = lax.dynamic_index_in_dim(x_pieces, piece_pos, 0, keepdims=False)
            h_in = jnp.where(stage_idx == 0, first_rows, recv)

            def run_piece(fwd_state):
                k_cur, v_cur, saved_cur, grad_cur, loss_cur = fwd_state
                h_out, key_rows, value_rows = stage_piece(h_in, params, k_cur, v_cur, row_start)
                k_cur = lax.dynamic_update_slice(k_cur, key_rows, (0, row_start, 0))
                v_cur = lax.dynamic_update_slice(v_cur, value_rows, (0, row_start, 0))
                saved_cur = lax.dynamic_update_index_in_dim(saved_cur, h_in, piece_pos, 0)
                target = lax.dynamic_index_in_dim(y_pieces, piece_pos, 0, keepdims=False)
                resid_err = h_out.astype(jnp.float32) - target.astype(jnp.float32)
                grad_cur = lax.dynamic_update_index_in_dim(grad_cur, (resid_err / norm_count).astype(jnp.bfloat16), piece_pos, 0)
                loss_cur = loss_cur + jnp.where(is_last, 0.5 * jnp.sum(resid_err * resid_err) / norm_count, 0.0)
                return h_out, (k_cur, v_cur, saved_cur, grad_cur, loss_cur)

            def skip_piece(fwd_state):
                return jnp.zeros(act_shape, jnp.bfloat16), fwd_state

            h_out, fwd_state = lax.cond(active, run_piece, skip_piece, (k_cache, v_cache, saved_in, top_grad, loss_acc))
            recv = lax.ppermute(h_out, 'stage', fwd_pairs)
            return (recv,) + fwd_state, None

        cache_zero = jnp.zeros((layers, seq_len, width), jnp.bfloat16)
        rows_zero = jnp.zeros((pieces,) + act_shape, jnp.bfloat16)
        fwd_init = (jnp.zeros(act_shape, jnp.bfloat16), cache_zero, cache_zero, rows_zero, rows_zero, jnp.zeros((), jnp.float32))
        fwd_final, fwd_rest = lax.scan(fwd_tick, fwd_init, jnp.arange(ticks))
        k_cache = fwd_final[1]
        v_cache = fwd_final[2]
        saved_in = fwd_final[3]
        top_grad = fwd_final[4]
        loss_acc = fwd_final[5]

        def bwd_tick(carry, tick_idx):
            recv, dk_acc, dv_acc, grad_acc = carry
            piece_idx = pieces - 1 - tick_idx + (stages - 1 - stage_idx)
            active = (piece_idx >= 0) & (piece_idx < pieces)
            piece_pos = jnp.clip(piece_idx, 0, pieces - 1)
            row_start = piece_pos * PIECE_LEN
            top_rows = lax.dynamic_index_in_dim(top_grad, piece_pos, 0, keepdims=False)
            dh_out = jnp.where(is_last, top_rows, recv)

            def run_piece(bwd_state):
                dk_cur, dv_cur, grad_cur = bwd_state
                h_in = lax.dynamic_index_in_dim(saved_in, piece_pos, 0, keepdims=False)
                fwd_outs, pullback = jax.vjp(lambda h_arg, p_arg, k_arg, v_arg: stage_piece(h_arg, p_arg, k_arg, v_arg, row_start), h_in, params, k_cache, v_cache)
                dk_own = lax.dynamic_slice(dk_cur, (0, row_start, 0), (layers, PIECE_LEN, width)).astype(jnp.bfloat16)
                dv_own = lax.dynamic_slice(dv_cur, (0, row_start, 0), (layers, PIECE_LEN, width)).astype(jnp.bfloat16)
                dh_in, d_params, d_kcache, d_vcache = pullback((dh_out, dk_own, dv_own))
                dk_cur = dk_cur + d_kcache.astype(jnp.float32)
                dv_cur = dv_cur + d_vcache.astype(jnp.float32)
                grad_cur = tuple(acc_part + grad_part.astype(jnp.float32) for acc_part, grad_part in zip(grad_cur, d_params))
                return dh_in, (dk_cur, dv_cur, grad_cur)

            def skip_piece(bwd_state):
                return jnp.zeros(act_shape, jnp.bfloat16), bwd_state

            dh_in, bwd_state = lax.cond(active, run_piece, skip_piece, (dk_acc, dv_acc, grad_acc))
            recv = lax.ppermute(dh_in, 'stage', bwd_pairs)
            return (recv,) + bwd_state, None

        acc_zero = jnp.zeros((layers, seq_len, width), jnp.float32)
        grad_zero = tuple(jnp.zeros(leaf.shape, jnp.float32) for leaf in params)
        bwd_init = (jnp.zeros(act_shape, jnp.bfloat16), acc_zero, acc_zero, grad_zero)
        bwd_final, bwd_rest = lax.scan(bwd_tick, bwd_init, jnp.arange(ticks))
        loss_total = lax.psum(loss_acc, 'stage')
        return (loss_total.reshape(1),) + bwd_final[3]

    weight_spec = P('stage')
    grad_spec = P(('data', 'stage'))
    return jax.shard_map(per_device, mesh=mesh, in_specs=(P('data'), P('data'), weight_spec, weight_spec, weight_spec, weight_spec, weight_spec), out_specs=(P('data'),) + (grad_spec,) * 5, check_vma=False)
```

profile of v0, /device:TPU:0, one launch (start us, length us, event | category | flops | bytes accessed | tf_op | source)
XLA Modules:
  0.0 2262.3 jit_solution(14917820776661163087)
XLA Ops:
  5.9 435.8 %while.47 = (s32[]{:T(128)}, bf16[256,1280]{1,0:T(8,128)(2,1)S(1)}, bf16[1,512,1280]{1,2,0:T(8,128)(2,1)}, bf16[1,512,1280]{1,2,0:T(8,128)(2,1)}, bf16[2,256,128...) while((s32[]{:T(128)}, bf16[256,1280]{1,0:T(8,128)(2,1)S(1)}, ...), condition=%wide.region_8.9_spmd, body=%wide.region_0.8_spmd.sunk | while | flops 10775891968 | bytes 140587312 | solution.py:107
  7.2 58.5 %conditional.4 = (bf16[256,1280]{1,0:T(8,128)(2,1)}, bf16[1,512,1280]{1,2,0:T(8,128)(2,1)}, bf16[1,512,1280]{1,2,0:T(8,128)(2,1)}, bf16[2,256,1280]{2,1,0:T(8,12...) conditional(s32[]{:T(128)} %convert_element_type.590, (bf16[1,512,1280]{1,2,0:T(8,128)(2,1)}, ...), branch_computations={%region_1.1_spmd, %region_2.7_spmd} | conditional | flops 10775891968 | bytes 137965440 | solution.py:100
  15.4 6.6 fusion.24
  28.1 8.9 fusion.193
  37.0 5.9 fusion.51
  45.1 17.8 fusion.58
  69.9 58.5 %conditional.4 = (bf16[256,1280]{1,0:T(8,128)(2,1)}, bf16[1,512,1280]{1,2,0:T(8,128)(2,1)}, bf16[1,512,1280]{1,2,0:T(8,128)(2,1)}, bf16[2,256,1280]{2,1,0:T(8,12...) conditional(s32[]{:T(128)} %convert_element_type.590, (bf16[1,512,1280]{1,2,0:T(8,128)(2,1)}, ...), branch_computations={%region_1.1_spmd, %region_2.7_spmd} | conditional | flops 10775891968 | bytes 137965440 | solution.py:100
  78.1 6.6 fusion.24
  90.8 8.9 fusion.193
  99.7 5.9 fusion.51
  107.9 17.8 fusion.58
  134.5 65.3 %collective-permute-start = (bf16[256,1280]{1,0:T(8,128)(2,1)}, bf16[256,1280]{1,0:T(8,128)(2,1)S(1)}, u32[]{:S(2)}, u32[]{:S(2)}) collective-permute-start(bf16[256,1280]{1,0:T(8,128)(2,1)} %get-tuple-element.1110), channel_id=1, source_target_pairs={{0,1},{1,2},{2,3},{3,4},{4,5},{5,6},{6,7}} | collective-permute-start | bytes 1966088 | tf_op jit(solution)/shard_map/while/body/eval_jaxpr/ppermute | solution.py:101
  203.6 10.2 collective-permute-start
  217.7 67.8 %collective-permute-start = (bf16[256,1280]{1,0:T(8,128)(2,1)}, bf16[256,1280]{1,0:T(8,128)(2,1)S(1)}, u32[]{:S(2)}, u32[]{:S(2)}) collective-permute-start(bf16[256,1280]{1,0:T(8,128)(2,1)} %get-tuple-element.1110), channel_id=1, source_target_pairs={{0,1},{1,2},{2,3},{3,4},{4,5},{5,6},{6,7}} | collective-permute-start | bytes 1966088 | tf_op jit(solution)/shard_map/while/body/eval_jaxpr/ppermute | solution.py:101
  289.3 10.2 collective-permute-start
  303.3 51.6 %collective-permute-start = (bf16[256,1280]{1,0:T(8,128)(2,1)}, bf16[256,1280]{1,0:T(8,128)(2,1)S(1)}, u32[]{:S(2)}, u32[]{:S(2)}) collective-permute-start(bf16[256,1280]{1,0:T(8,128)(2,1)} %get-tuple-element.1110), channel_id=1, source_target_pairs={{0,1},{1,2},{2,3},{3,4},{4,5},{5,6},{6,7}} | collective-permute-start | bytes 1966088 | tf_op jit(solution)/shard_map/while/body/eval_jaxpr/ppermute | solution.py:101
  358.7 10.2 collective-permute-start
  372.8 67.1 %collective-permute-start = (bf16[256,1280]{1,0:T(8,128)(2,1)}, bf16[256,1280]{1,0:T(8,128)(2,1)S(1)}, u32[]{:S(2)}, u32[]{:S(2)}) collective-permute-start(bf16[256,1280]{1,0:T(8,128)(2,1)} %get-tuple-element.1110), channel_id=1, source_target_pairs={{0,1},{1,2},{2,3},{3,4},{4,5},{5,6},{6,7}} | collective-permute-start | bytes 1966088 | tf_op jit(solution)/shard_map/while/body/eval_jaxpr/ppermute | solution.py:101
  441.8 189.4 %psum.7 = f32[1]{0:T(128)} all-reduce(f32[1]{0:T(128)} %bitcast.53), channel_id=1, replica_groups=mesh['data'=1,'stage'=8] {'stage'}, use_global_device_ids=true, to_apply=%region_9.10 | all-reduce | flops 1 | bytes 8 | tf_op jit(solution)/shard_map/psum | solution.py:146
  638.1 8.4 broadcast_in_dim.125
  646.5 11.0 broadcast_in_dim.128
  657.4 12.6 broadcast_in_dim.127
  670.0 1591.3 %while.48 = (s32[]{:T(128)}, bf16[256,1280]{1,0:T(8,128)(2,1)S(1)}, f32[1,512,1280]{1,2,0:T(8,128)}, f32[1,512,1280]{1,2,0:T(8,128)}, f32[1,1280,3840]{2,1,0:T(8...) while((s32[]{:T(128)}, bf16[256,1280]{1,0:T(8,128)(2,1)S(1)}, ...), condition=%wide.region_22.23_spmd, body=%wide.region_10.22_spmd.sunk | while | flops 29048662016 | bytes 529770592 | solution.py:145
  703.9 10.8 collective-permute-done.1
  718.8 10.6 collective-permute-done.1
  733.5 10.6 collective-permute-done.1
  748.2 10.6 collective-permute-done.1
  763.0 10.6 collective-permute-done.1
  777.7 1132.8 %collective-permute-done.1 = bf16[256,1280]{1,0:T(8,128)(2,1)S(1)} collective-permute-done((bf16[256,1280]{1,0:T(8,128)(2,1)}, bf16[256,1280]{1,0:T(8,128)(2,1)S(1)}, u32[]{:S(2)}, u32[]{:S(2)}) %collective-permute-start.1) | collective-permute-done | bytes 655392 | tf_op jit(solution)/shard_map/while/body/eval_jaxpr/ppermute | solution.py:139
  1912.4 165.2 %conditional.5 = (bf16[256,1280]{1,0:T(8,128)(2,1)}, f32[1,512,1280]{1,2,0:T(8,128)}, f32[1,512,1280]{1,2,0:T(8,128)}, f32[1,1280,3840]{2,1,0:T(8,128)}, f32[1,1...) conditional(s32[]{:T(128)} %convert_element_type.591, ...), branch_computations={%region_11.11_spmd, %region_12.21_spmd} | conditional | flops 29048662016 | bytes 527148640 | solution.py:138
  1919.7 6.8 fusion.111
  1932.4 9.1 fusion.192
  1941.6 4.9 divide_convert_fusion.4
  1952.8 6.7 fusion.77
  1961.9 8.9 fusion.98
  1970.7 8.5 multiply_reduce_fusion.2
  1984.6 3.9 convolution_convert_fusion.6
  1988.5 5.3 fusion.87
  1994.6 4.0 convolution_convert_fusion.7
  1998.7 3.7 convolution_convert_fusion.5
  2004.6 7.1 fusion.153
  2014.2 5.9 convert_add_fusion.4
  2020.1 6.7 convert_add_fusion.3
  2026.7 14.1 convert_add_fusion.2
  2040.8 18.9 convert_add_fusion
  2059.7 17.9 convert_add_fusion.1
  2078.9 11.3 collective-permute-done.1
  2092.2 165.2 %conditional.5 = (bf16[256,1280]{1,0:T(8,128)(2,1)}, f32[1,512,1280]{1,2,0:T(8,128)}, f32[1,512,1280]{1,2,0:T(8,128)}, f32[1,1280,3840]{2,1,0:T(8,128)}, f32[1,1...) conditional(s32[]{:T(128)} %convert_element_type.591, ...), branch_computations={%region_11.11_spmd, %region_12.21_spmd} | conditional | flops 29048662016 | bytes 527148640 | solution.py:138
  2099.4 6.8 fusion.111
  2112.2 9.1 fusion.192
  2121.4 4.9 divide_convert_fusion.4
  2132.6 6.7 fusion.77
  2141.7 8.9 fusion.98
  2150.5 8.5 multiply_reduce_fusion.2
  2164.3 3.9 convolution_convert_fusion.6
  2168.2 5.3 fusion.87
  2174.4 4.0 convolution_convert_fusion.7
  2178.4 3.7 convolution_convert_fusion.5
  2184.4 7.0 fusion.153
  2193.9 5.9 convert_add_fusion.4
  2199.7 6.7 convert_add_fusion.3
  2206.4 14.1 convert_add_fusion.2
  2220.5 18.9 convert_add_fusion
  2239.4 17.9 convert_add_fusion.1
  (268 shorter events, 191.8 us)
Async XLA Ops:
  15.2 6.8 copy-start.8
  23.8 2.5 copy-start.10
  26.3 1.8 copy-start.11
  28.1 8.9 copy-start.12
  37.0 5.9 copy-start.9
  37.0 5.9 copy-start.17
  43.0 2.2 copy-start.15
  65.7 3.0 collective-permute-start
  77.9 6.8 copy-start.8
  86.5 2.5 copy-start.10
  89.0 1.8 copy-start.11
  90.8 8.9 copy-start.12
  99.7 5.9 copy-start.9
  99.7 5.9 copy-start.17
  105.7 2.2 copy-start.15
  128.4 4.0 collective-permute-start
  134.5 67.0 %collective-permute-start = (bf16[256,1280]{1,0:T(8,128)(2,1)}, bf16[256,1280]{1,0:T(8,128)(2,1)S(1)}, u32[]{:S(2)}, u32[]{:S(2)}) collective-permute-start(bf16[256,1280]{1,0:T(8,128)(2,1)} %get-tuple-element.1110), channel_id=1, source_target_pairs={{0,1},{1,2},{2,3},{3,4},{4,5},{5,6},{6,7}} | collective-permute-start | bytes 1966088 | tf_op jit(solution)/shard_map/while/body/eval_jaxpr/ppermute | solution.py:101
  203.6 11.9 collective-permute-start
  217.7 69.5 %collective-permute-start = (bf16[256,1280]{1,0:T(8,128)(2,1)}, bf16[256,1280]{1,0:T(8,128)(2,1)S(1)}, u32[]{:S(2)}, u32[]{:S(2)}) collective-permute-start(bf16[256,1280]{1,0:T(8,128)(2,1)} %get-tuple-element.1110), channel_id=1, source_target_pairs={{0,1},{1,2},{2,3},{3,4},{4,5},{5,6},{6,7}} | collective-permute-start | bytes 1966088 | tf_op jit(solution)/shard_map/while/body/eval_jaxpr/ppermute | solution.py:101
  289.3 11.9 collective-permute-start
  303.3 53.3 %collective-permute-start = (bf16[256,1280]{1,0:T(8,128)(2,1)}, bf16[256,1280]{1,0:T(8,128)(2,1)S(1)}, u32[]{:S(2)}, u32[]{:S(2)}) collective-permute-start(bf16[256,1280]{1,0:T(8,128)(2,1)} %get-tuple-element.1110), channel_id=1, source_target_pairs={{0,1},{1,2},{2,3},{3,4},{4,5},{5,6},{6,7}} | collective-permute-start | bytes 1966088 | tf_op jit(solution)/shard_map/while/body/eval_jaxpr/ppermute | solution.py:101
  358.7 11.9 collective-permute-start
  372.8 68.8 %collective-permute-start = (bf16[256,1280]{1,0:T(8,128)(2,1)}, bf16[256,1280]{1,0:T(8,128)(2,1)S(1)}, u32[]{:S(2)}, u32[]{:S(2)}) collective-permute-start(bf16[256,1280]{1,0:T(8,128)(2,1)} %get-tuple-element.1110), channel_id=1, source_target_pairs={{0,1},{1,2},{2,3},{3,4},{4,5},{5,6},{6,7}} | collective-permute-start | bytes 1966088 | tf_op jit(solution)/shard_map/while/body/eval_jaxpr/ppermute | solution.py:101
  695.8 4.0 collective-permute-start.1
  702.6 12.1 collective-permute-start.1
  717.5 11.9 collective-permute-start.1
  732.2 11.9 collective-permute-start.1
  746.9 11.9 collective-permute-start.1
  761.7 11.9 collective-permute-start.1
  776.4 1134.1 %collective-permute-start.1 = (bf16[256,1280]{1,0:T(8,128)(2,1)}, bf16[256,1280]{1,0:T(8,128)(2,1)S(1)}, u32[]{:S(2)}, u32[]{:S(2)}) collective-permute-start(bf16[256,1280]{1,0:T(8,128)(2,1)} %get-tuple-element.1137), channel_id=1, source_target_pairs={{1,0},{2,1},{3,2},{4,3},{5,4},{6,5},{7,6}} | collective-permute-start | bytes 1966088 | tf_op jit(solution)/shard_map/while/body/eval_jaxpr/ppermute | solution.py:139
  1946.4 2.7 copy-start
  1946.4 4.1 copy-start.18
  1949.1 3.6 copy-start.5
  1959.5 2.4 copy-start.1
  1970.7 8.5 copy-start.7
  1979.6 0.8 copy-start.2
  1984.5 3.9 copy-start.4
  1984.6 9.3 slice-start
  1988.4 5.4 slice-start.1
  1988.4 5.9 slice-start.2
  1988.4 6.2 copy-start.13
  1994.6 4.0 copy-start.14
  2004.6 7.1 copy-start.3
  2014.2 5.9 copy-start.6
  2077.6 12.6 collective-permute-start.1
  2126.2 2.7 copy-start
  2126.2 4.1 copy-start.18
  2128.9 3.6 copy-start.5
  2139.3 2.4 copy-start.1
  2150.5 8.5 copy-start.7
  2159.4 0.8 copy-start.2
  2164.3 3.9 copy-start.4
  2164.3 9.3 slice-start
  2168.2 5.4 slice-start.1
  2168.2 5.9 slice-start.2
  2168.2 6.2 copy-start.13
  2174.4 4.0 copy-start.14
  2184.3 7.1 copy-start.3
  2193.8 5.9 copy-start.6
  2257.4 4.0 collective-permute-start.1
  2261.3 0.6 copy-start.16
where the time goes:
time: 2280 us; the launch traced here: 2260 us
  waiting for transfers between devices  1220 us (54%)
  matrix products  338 us (15%)
  starting transfers between devices  298 us (13%)
  blocking collectives  189 us (8%)
  local copies, waits for them, and re-layouts  132 us (6%)
  other arithmetic  48.8 us (2%)
  loops' own time  37.8 us (2%)
    ppermute x9, waiting for transfers between devices, bwd_tick(): recv = lax.ppermute(dh_in, 'stage', bwd_pairs)  1200 us
    ppermute x9, starting transfers between devices, fwd_tick(): recv = lax.ppermute(h_out, 'stage', fwd_pairs)  286 us
    psum x1, blocking collectives, per_device(): loss_total = lax.psum(loss_acc, 'stage')  189 us
    dot_general x6, matrix products, stage_piece(): jnp.dot(act_bf, w_down[layer_idx], preferred_element_type=jnp.float32)  91.1 us
    dot_general x8, matrix products, stage_piece(): jnp.dot(normed, w_qkv[layer_idx], preferred_element_type=jnp.float32)  69.2 us
    dot_general x6, matrix products, stage_piece(): upper = jnp.dot(normed, w_up[layer_idx], preferred_element_type=jnp.float32)  66.3 us
  transfers between devices with their start and end apart: 18, of which 18 were waited for; matrix products, arithmetic and copies ran while one was open for 0% of the time, Pallas kernels for 0%

commit v1 on v0

v1 whole, which is shorter than its diff:
```python
import functools
import math

import jax
import jax.numpy as jnp
from jax import lax
from jax.experimental import pallas as pl
from jax.experimental.pallas import tpu as pltpu
from jax.sharding import PartitionSpec as P

MESH = pl.DeviceIdType.MESH
BF = jnp.bfloat16
F32 = jnp.float32
HEAD_DIM = 64
ROWS = 256
EPS = 1e-6
GELU_C = math.sqrt(2.0 / math.pi)
GELU_A = 0.044715
LOG2E = math.log2(math.e)


def dot_nn(a, b):
    return jnp.dot(a, b, preferred_element_type=F32)


def dot_nt(a, b):
    return lax.dot_general(a, b, (((1,), (1,)), ((), ())), preferred_element_type=F32)


def dot_tn(a, b):
    return lax.dot_general(a, b, (((0,), (0,)), ((), ())), preferred_element_type=F32)


def norm_stats(h_bf):
    h = h_bf.astype(F32)
    inv = lax.rsqrt(jnp.mean(h * h, axis=-1, keepdims=True) + EPS)
    return h, inv


def norm_grad(dn, h_bf, gain):
    h, inv = norm_stats(h_bf)
    hhat = h * inv
    dgain = jnp.sum(dn * hhat, axis=0, keepdims=True)
    dhhat = dn * gain
    corr = jnp.mean(dhhat * hhat, axis=-1, keepdims=True)
    return inv * (dhhat - hhat * corr), dgain


def gelu_parts(u):
    u2 = u * u
    t = jnp.tanh(u * (GELU_C + (GELU_C * GELU_A) * u2))
    return u2, t


def pipeline_kernel(stages, seq, width, x_ref, y_ref, wqkv, wout, wup, wdown, gain_ref,
                    loss_ref, dgain_ref, n1_o, a_o, n2_o, act_o, du_o, dqkv_o, dhm_o, dho_o,
                    ring, hin, hs, hmid, n1, att, n2, qkv, u_buf, act, acc, dho, dhs, dhm, da, du, dqkv, dkv, bias, loss_in,
                    wsem, xsem, osem, fs, fr, bs, br, ls, lr):
    me = lax.axis_index('stage')
    data = lax.axis_index('data')
    last = stages - 1
    right = lax.rem(me + 1, stages)
    left = lax.rem(me + stages - 1, stages)
    D = width
    CH = D
    pairs = D // (2 * HEAD_DIM)
    ffn_chunks = wup.shape[2] // CH
    count = float(seq * width)

    def src(kind, j):
        cols = pl.ds(pl.multiple_of(j * CH, CH), CH)
        if kind == 'q':
            return wqkv.at[0, :, cols]
        if kind == 'o':
            return wout.at[0]
        if kind == 'u':
            return wup.at[0, :, cols]
        return wdown.at[0, cols, :]

    def fetch(kind, j, slot):
        pltpu.make_async_copy(src(kind, j), ring.at[slot], wsem.at[slot]).start()

    def arrived(slot):
        pltpu.make_async_copy(wout.at[0], ring.at[slot], wsem.at[slot]).wait()

    def put(idx, p, buf, out):
        return pltpu.make_async_copy(buf, out.at[pl.ds(pl.multiple_of(p * ROWS, ROWS), ROWS)], osem.at[idx, p])

    def fwd_copy(p):
        return pltpu.make_async_remote_copy(src_ref=hs.at[p], dst_ref=hin.at[p], send_sem=fs.at[p], recv_sem=fr.at[p],
                                            device_id=(data, right), device_id_type=MESH)

    def bwd_copy(p):
        return pltpu.make_async_remote_copy(src_ref=dhs.at[p], dst_ref=dho.at[p], send_sem=bs.at[p], recv_sem=br.at[p],
                                            device_id=(data, left), device_id_type=MESH)

    def loss_copy():
        return pltpu.make_async_remote_copy(src_ref=loss_in, dst_ref=loss_in, send_sem=ls.at[0], recv_sem=lr.at[0],
                                            device_id=(data, left), device_id_type=MESH)

    fetch('q', 0, 0)
    fetch('q', 1, 1)
    fetch('q', 2, 2)
    fetch('o', 0, 3)

    @pl.when(me == 0)
    def _():
        for p in range(2):
            pltpu.make_async_copy(x_ref.at[0, pl.ds(p * ROWS, ROWS)], hin.at[p], xsem.at[p]).start()

    @pl.when(me == last)
    def _():
        for p in range(2):
            pltpu.make_async_copy(y_ref.at[0, pl.ds(p * ROWS, ROWS)], dho.at[p], xsem.at[p]).start()

    barrier = pltpu.get_barrier_semaphore()
    for nb in (left, right):
        pl.semaphore_signal(barrier, inc=1, device_id=(data, nb), device_id_type=MESH)
    pl.semaphore_wait(barrier, 2)

    dgain_ref[...] = jnp.zeros_like(dgain_ref)

    @pl.when(me == last)
    def _():
        loss_in[...] = jnp.zeros_like(loss_in)
    qkv[pl.ds(ROWS, ROWS), pl.ds(D, 2 * D)] = jnp.zeros((ROWS, 2 * D), BF)
    gain0 = gain_ref[0, 0:1, :].astype(F32)
    gain1 = gain_ref[0, 1:2, :].astype(F32)
    low = lax.broadcasted_iota(jnp.int32, (ROWS, 2 * HEAD_DIM), 1) < HEAD_DIM

    def set_bias(p):
        r = lax.broadcasted_iota(jnp.int32, (ROWS, seq), 0) + p * ROWS
        c = lax.broadcasted_iota(jnp.int32, (ROWS, seq), 1)
        bias[...] = jnp.where(c <= r, 0.0, -1e30)

    def probs(qh, k):
        s = dot_nt(qh, k) * (HEAD_DIM ** -0.5 * LOG2E) + bias[...]
        e = jnp.exp2(s - jnp.max(s, axis=-1, keepdims=True))
        return e * (1.0 / jnp.sum(e, axis=-1, keepdims=True))

    def fwd_piece(p, carry):
        row0 = pl.multiple_of(p * ROWS, ROWS)
        rows = pl.ds(row0, ROWS)
        set_bias(p)

        @pl.when(me == 0)
        def _():
            pltpu.make_async_copy(x_ref.at[0, rows], hin.at[p], xsem.at[p]).wait()

        @pl.when(me > 0)
        def _():
            fwd_copy(p).wait_recv()

        h, inv = norm_stats(hin[p])
        n1[p] = (h * inv * gain0).astype(BF)
        put(0, p, n1.at[p], n1_o).start()

        @pl.loop(0, 3)
        def _(c):
            arrived(c)
            cols = pl.ds(pl.multiple_of(c * CH, CH), CH)
            qkv[rows, cols] = dot_nn(n1[p], ring[c]).astype(BF)

            @pl.when(c == 0)
            def _():
                fetch('u', 0, 0)

            @pl.when(c == 1)
            def _():
                fetch('d', 0, 1)

            @pl.when(c == 2)
            def _():
                fetch('u', 1, 2)

        @pl.loop(0, pairs)
        def _(i):
            co = pl.multiple_of(i * 2 * HEAD_DIM, 2 * HEAD_DIM)
            q = qkv[rows, pl.ds(co, 2 * HEAD_DIM)]
            k = qkv[:, pl.ds(D + co, 2 * HEAD_DIM)]
            v = qkv[:, pl.ds(2 * D + co, 2 * HEAD_DIM)]
            zero = jnp.zeros_like(q)
            outs = []
            for qh in (jnp.where(low, q, zero), jnp.where(low, zero, q)):
                outs.append(dot_nn(probs(qh, k).astype(BF), v))
            att[p, :, pl.ds(co, 2 * HEAD_DIM)] = jnp.where(low, outs[0], outs[1]).astype(BF)

        put(1, p, att.at[p], a_o).start()
        arrived(3)
        hmid[p] = (hin[p].astype(F32) + dot_nn(att[p], ring[3])).astype(BF)
        fetch('d', 1, 3)
        h, inv = norm_stats(hmid[p])
        n2[p] = (h * inv * gain1).astype(BF)
        put(2, p, n2.at[p], n2_o).start()
        acc[...] = hmid[p].astype(F32)

        @pl.loop(0, ffn_chunks)
        def _(j):
            cols = pl.ds(pl.multiple_of(j * CH, CH), CH)
            s0 = lax.rem(2 * j, 4)
            arrived(s0)
            u = dot_nn(n2[p], ring[s0])
            u_buf[rows, cols] = u

            @pl.when(j < 2)
            def _():
                fetch('u', j + 2, s0)

            @pl.when((j >= 2) & (p == 0))
            def _():
                fetch('q', (j - 2) * 2, s0)

            @pl.when((j >= 2) & (p == 1))
            def _():
                fetch('d', j - 2, s0)
            u2, t = gelu_parts(u_buf[rows, cols])
            act[p, :, cols] = (0.5 * u_buf[rows, cols] * (1.0 + t)).astype(BF)
            s1 = s0 + 1
            arrived(s1)
            acc[...] += dot_nn(act[p, :, cols], ring[s1])

            @pl.when(j < 2)
            def _():
                fetch('d', j + 2, s1)

            @pl.when((j == 2) & (p == 0))
            def _():
                fetch('q', 1, s1)

            @pl.when((j == 3) & (p == 0))
            def _():
                fetch('o', 0, s1)

            @pl.when((j >= 2) & (p == 1))
            def _():
                fetch('u', j - 2, s1)

        hs[p] = acc[...].astype(BF)

        @pl.when(me < last)
        def _():
            fwd_copy(p).start()

        put(3, p, act.at[p], act_o).start()

        @pl.when(me == last)
        def _():
            pltpu.make_async_copy(y_ref.at[0, rows], dho.at[p], xsem.at[p]).wait()
            err = hs[p].astype(F32) - dho[p].astype(F32)
            dho[p] = (err / count).astype(BF)
            part = jnp.sum(jnp.sum(err * err, axis=0, keepdims=True), axis=1, keepdims=True)
            loss_in[...] += part * (0.5 / count)
        return carry

    lax.fori_loop(0, 2, fwd_piece, 0)

    def bwd_piece(t, carry):
        p = 1 - t
        row0 = pl.multiple_of(p * ROWS, ROWS)
        rows = pl.ds(row0, ROWS)
        set_bias(p)

        @pl.when(me < last)
        def _():
            bwd_copy(p).wait_recv()

        @pl.when((me < last) & (t == 0))
        def _():
            loss_copy().wait_recv()

        @pl.when((me > 0) & (t == 0))
        def _():
            loss_copy().start()
        put(7, p, dho.at[p], dho_o).start()
        acc[...] = jnp.zeros_like(acc)

        @pl.loop(0, ffn_chunks)
        def _(j):
            cols = pl.ds(pl.multiple_of(j * CH, CH), CH)
            s0 = lax.rem(2 * j, 4)
            arrived(s0)
            dact = dot_nt(dho[p], ring[s0])

            @pl.when(j < 2)
            def _():
                fetch('d', j + 2, s0)

            @pl.when(j == 2)
            def _():
                fetch('o', 0, s0)

            @pl.when(j == 3)
            def _():
                fetch('q', 1, s0)
            u = u_buf[rows, cols]
            u2, th = gelu_parts(u)
            slope = 0.5 * (1.0 + th) + (0.5 * u) * (1.0 - th * th) * (GELU_C + (3.0 * GELU_C * GELU_A) * u2)
            du[p, :, cols] = (dact * slope).astype(BF)
            s1 = s0 + 1
            arrived(s1)
            acc[...] += dot_nt(du[p, :, cols], ring[s1])

            @pl.when(j < 2)
            def _():
                fetch('u', j + 2, s1)

            @pl.when(j == 2)
            def _():
                fetch('q', 0, s1)

            @pl.when(j == 3)
            def _():
                fetch('q', 2, s1)

        put(4, p, du.at[p], du_o).start()
        dh, dg = norm_grad(acc[...], hmid[p], gain1)
        dgain_ref[1:2, :] += dg
        dhm[p] = (dho[p].astype(F32) + dh).astype(BF)
        put(6, p, dhm.at[p], dhm_o).start()
        arrived(0)
        da[...] = dot_nt(dhm[p], ring[0]).astype(BF)

        @pl.when(t == 0)
        def _():
            fetch('d', 0, 0)

        @pl.loop(0, pairs)
        def _(i):
            co = pl.multiple_of(i * 2 * HEAD_DIM, 2 * HEAD_DIM)
            lanes = pl.ds(co, 2 * HEAD_DIM)
            q = qkv[rows, lanes]
            k = qkv[:, pl.ds(D + co, 2 * HEAD_DIM)]
            v = qkv[:, pl.ds(2 * D + co, 2 * HEAD_DIM)]
            do = da[:, lanes]
            prod = do.astype(F32) * att[p, :, lanes].astype(F32)
            zero = jnp.zeros_like(q)
            dqs = []
            dk = jnp.zeros((seq, 2 * HEAD_DIM), F32)
            dv = jnp.zeros((seq, 2 * HEAD_DIM), F32)
            for hh in range(2):
                sel = low if hh == 0 else jnp.logical_not(low)
                qh = jnp.where(sel, q, zero)
                doh = jnp.where(sel, do, zero)
                pr = probs(qh, k)
                dp = dot_nt(doh, v)
                delta = jnp.sum(jnp.where(sel, prod, 0.0), axis=-1, keepdims=True)
                ds = (pr * (dp - delta) * (HEAD_DIM ** -0.5)).astype(BF)
                dqs.append(dot_nn(ds, k))
                dk = dk + dot_tn(ds, qh)
                dv = dv + dot_tn(pr.astype(BF), doh)
            dqkv[p, :, lanes] = jnp.where(low, dqs[0], dqs[1]).astype(BF)
            klanes = pl.ds(D + co, 2 * HEAD_DIM)
            vlanes = pl.ds(2 * D + co, 2 * HEAD_DIM)

            @pl.when(t == 0)
            def _():
                dqkv[p, :, klanes] = dk[ROWS:].astype(BF)
                dqkv[p, :, vlanes] = dv[ROWS:].astype(BF)
                dkv[:, lanes] = dk[:ROWS]
                dkv[:, klanes] = dv[:ROWS]

            @pl.when(t == 1)
            def _():
                dqkv[p, :, klanes] = (dk[:ROWS] + dkv[:, lanes]).astype(BF)
                dqkv[p, :, vlanes] = (dv[:ROWS] + dkv[:, klanes]).astype(BF)

        put(5, p, dqkv.at[p], dqkv_o).start()
        acc[...] = jnp.zeros_like(acc)

        @pl.loop(0, 3)
        def _(c):
            arrived(c + 1)
            cols = pl.ds(pl.multiple_of(c * CH, CH), CH)
            acc[...] += dot_nt(dqkv[p, :, cols], ring[c + 1])

            @pl.when((c == 0) & (t == 0))
            def _():
                fetch('u', 0, 1)

            @pl.when((c == 1) & (t == 0))
            def _():
                fetch('d', 1, 2)

            @pl.when((c == 2) & (t == 0))
            def _():
                fetch('u', 1, 3)

        dh, dg = norm_grad(acc[...], hin[p], gain0)
        dgain_ref[0:1, :] += dg

        @pl.when(me > 0)
        def _():
            dhs[p] = (dhm[p].astype(F32) + dh).astype(BF)
            bwd_copy(p).start()
        return carry

    lax.fori_loop(0, 2, bwd_piece, 0)
    loss_ref[...] = loss_in[...]

    for p in range(2):
        for idx, (buf, out) in enumerate(((n1, n1_o), (att, a_o), (n2, n2_o), (act, act_o), (du, du_o), (dqkv, dqkv_o), (dhm, dhm_o), (dho, dho_o))):
            put(idx, p, buf.at[p], out).wait()

        @pl.when(me < last)
        def _():
            fwd_copy(p).wait_send()

        @pl.when(me > 0)
        def _():
            bwd_copy(p).wait_send()

    @pl.when(me > 0)
    def _():
        loss_copy().wait_send()


def run_pipeline(stages, x, y, w_qkv, w_out, w_up, w_down, gain):
    seq, width = x.shape[1], x.shape[2]
    ffn = w_up.shape[2]
    hbm = pl.BlockSpec(memory_space=pl.ANY)
    vmem = pl.BlockSpec(memory_space=pltpu.VMEM)
    V = pltpu.VMEM
    piece = (2, ROWS, width)
    widths = (width, width, width, ffn, ffn, 3 * width, width, width)
    outs = [jax.ShapeDtypeStruct((8, 128), F32), jax.ShapeDtypeStruct((2, width), F32)]
    outs += [jax.ShapeDtypeStruct((seq, w), BF) for w in widths]
    dma = pltpu.SemaphoreType.DMA
    return pl.pallas_call(
        functools.partial(pipeline_kernel, stages, seq, width),
        out_shape=outs,
        in_specs=[hbm] * 6 + [vmem],
        out_specs=[vmem, vmem] + [hbm] * 8,
        scratch_shapes=[
            V((4, width, width), BF),
            V(piece, BF), V(piece, BF), V(piece, BF),
            V(piece, BF), V(piece, BF), V(piece, BF),
            V((seq, 3 * width), BF),
            V((seq, ffn), F32),
            V((2, ROWS, ffn), BF),
            V((ROWS, width), F32),
            V(piece, BF), V(piece, BF), V(piece, BF), V((ROWS, width), BF),
            V((2, ROWS, ffn), BF), V((2, ROWS, 3 * width), BF),
            V((ROWS, 2 * width), F32),
            V((ROWS, seq), F32), V((8, 128), F32),
            dma((4,)), dma((2,)), dma((8, 2)),
            dma((2,)), dma((2,)), dma((2,)), dma((2,)), dma((1,)), dma((1,)),
        ],
        compiler_params=pltpu.CompilerParams(collective_id=0, has_side_effects=True, vmem_limit_bytes=67043328),
        name='pipeline',
    )(x, y, w_qkv, w_out, w_up, w_down, gain)


def solution(mesh):
    stages = mesh.shape['stage']

    def per_device(x, y, w_qkv, w_out, w_up, w_down, norm_gain):
        loss, dgain, n1, att, n2, act, du, dqkv, dhm, dho = run_pipeline(stages, x, y, w_qkv, w_out, w_up, w_down, norm_gain)
        g_qkv = dot_tn(n1, dqkv)
        g_out = dot_tn(att, dhm)
        g_up = dot_tn(n2, du)
        g_down = dot_tn(act, dho)
        return loss[0, 0].reshape(1), g_qkv[None], g_out[None], g_up[None], g_down[None], dgain[None]

    weight_spec = P('stage')
    grad_spec = P(('data', 'stage'))
    return jax.shard_map(per_device, mesh=mesh, in_specs=(P('data'), P('data')) + (weight_spec,) * 5,
                         out_specs=(P('data'),) + (grad_spec,) * 5, check_vma=False)
```

time: 2280 us -> 613 us (0.27)
  waiting for transfers between devices: 1220 us -> 0 us
  Pallas kernels: 0 us -> 568 us
  starting transfers between devices: 298 us -> 0 us
  matrix products: 338 us -> 42.8 us
  blocking collectives: 189 us -> 0 us
  local copies, waits for them, and re-layouts: 132 us -> 1.82 us
  other arithmetic: 48.8 us -> 0 us
  loops' own time: 37.8 us -> 0 us
    ppermute x18 -> x0, waiting for transfers between devices: 1220 us -> none  [the longest x9 1200 us: bwd_tick(): recv = lax.ppermute(dh_in, 'stage', bwd_pairs)]
    pallas_call x0 -> x1, Pallas kernels: none -> 568 us  [run_pipeline(): pl.pallas_call(functools.partial(pipeline_kernel, stages, seq, width), ou...]
    ppermute x18 -> x0, starting transfers between devices: 298 us -> none  [the longest x9 286 us: fwd_tick(): recv = lax.ppermute(h_out, 'stage', fwd_pairs)]
    dot_general x40 -> x4, matrix products: 302 us -> 42.8 us  [dot_tn(): lax.dot_general(a, b, (((0,), (0,)), ((), ())), preferred_element_type=F32)]
    psum x1 -> x0, blocking collectives: 189 us -> none  [per_device(): loss_total = lax.psum(loss_acc, 'stage')]
    broadcast_in_dim x11 -> x0, local copies, waits for them, and re-layouts: 43.5 us -> none  [the longest x5 35.1 us: per_device(): grad_zero = tuple((jnp.zeros(leaf.shape, jnp.float32) for leaf in params))]
    another operation x20 -> x0, loops' own time: 37.8 us -> none  [the longest x1 29 us: per_device(): bwd_final, bwd_rest = lax.scan(bwd_tick, bwd_init, jnp.arange(ticks))]
    sub x4 -> x0, matrix products: 36.1 us -> none  [attend(): probs_bf = jax.nn.softmax(scores, axis=-1).astype(jnp.bfloat16)]
  transfers between devices with their start and end apart: 18 -> 0, of which waited for: 18 -> 0; matrix products, arithmetic and copies ran while one was open for 0% -> 0% of each run, Pallas kernels for 0% -> 0%
where the time goes in v1:
time: 613 us
  Pallas kernels  568 us (93%)
  matrix products  42.8 us (7%)
    pallas_call x1, Pallas kernels, run_pipeline(): pl.pallas_call(functools.partial(pipeline_kernel, stages, seq, width), ou...  568 us
    dot_general x4, matrix products, dot_tn(): lax.dot_general(a, b, (((0,), (0,)), ((), ())), preferred_element_type=F32)  42.8 us

profile of v1, /device:TPU:0, one launch (start us, length us, event | category | flops | bytes accessed | tf_op | source)
XLA Modules:
  0.0 613.0 jit_solution(331259424278938043)
XLA Ops:
  0.6 567.7 %pipeline.1 = (f32[8,128]{1,0:T(8,128)}, f32[2,1280]{1,0:T(2,128)}, bf16[512,1280]{1,0:T(8,128)(2,1)}, bf16[512,1280]{1,0:T(8,128)(2,1)}, bf16[512,1280]{1,0:T(8...) custom-call(bf16[1,512,1280]{2,1,0:T(8,128)(2,1)} %x_ref.1, ...), custom_call_target="tpu_custom_call" | custom-call | tf_op jit(solution)/shard_map/pipeline/pallas_call | solution.py:428
  568.4 0.0 copy-start.1
  568.4 0.0 copy-start.6
  568.4 15.3 %convolution_bitcast_fusion = f32[1,5120,1280]{2,1,0:T(8,128)} fusion(bf16[512,5120]{1,0:T(8,128)(2,1)} %get-tuple-element.23, bf16[512,1280]{1,0:T(8,128)(2,1)} %get-tuple-element.24), kind=kOutput, calls=%fused_computation | convolution fusion | flops 6710886400 | bytes 32768000 | tf_op jit(solution)/shard_map/dot_general | solution.py:31
  583.7 0.0 copy-done.1
  583.7 0.0 copy-done.6
  583.7 0.0 copy-start.4
  583.7 0.0 copy-start.5
  583.7 12.9 %convolution_bitcast_fusion.1 = f32[1,1280,5120]{2,1,0:T(8,128)} fusion(bf16[512,1280]{1,0:T(8,128)(2,1)S(1)} %copy-done.6, bf16[512,5120]{1,0:T(8,128)(2,1)S(1)} %copy-done.1), kind=kOutput, calls=%fused_computation.1 | convolution fusion | flops 6710886400 | bytes 32768000 | tf_op jit(solution)/shard_map/dot_general | solution.py:31
  596.6 0.0 copy-done.4
  596.6 0.0 copy-done.5
  596.6 0.0 copy-start.2
  596.7 0.0 copy-start.3
  596.7 4.7 convolution_bitcast_fusion.3
  601.4 0.0 copy-done.2
  601.4 0.0 copy-done.3
  601.4 0.0 copy-start
  601.4 9.9 %convolution_bitcast_fusion.2 = f32[1,1280,3840]{2,1,0:T(8,128)} fusion(bf16[512,1280]{1,0:T(8,128)(2,1)S(1)} %copy-done.3, bf16[512,3840]{1,0:T(8,128)(2,1)S(1)} %copy-done.2), kind=kOutput, calls=%fused_computation.2 | convolution fusion | flops 5033164800 | bytes 24903680 | tf_op jit(solution)/shard_map/dot_general | solution.py:31
  611.2 1.2 slice.3
  612.4 0.0 copy-done
  612.4 0.6 copy.14
Async XLA Ops:
  568.4 15.3 %copy-start.1 = (bf16[512,5120]{1,0:T(8,128)(2,1)S(1)}, bf16[512,5120]{1,0:T(8,128)(2,1)}, u32[]{:S(2)}) copy-start(bf16[512,5120]{1,0:T(8,128)(2,1)} %get-tuple-element.22) | copy-start | bytes 15728644
  568.4 15.3 %copy-start.6 = (bf16[512,1280]{1,0:T(8,128)(2,1)S(1)}, bf16[512,1280]{1,0:T(8,128)(2,1)}, u32[]{:S(2)}) copy-start(bf16[512,1280]{1,0:T(8,128)(2,1)} %get-tuple-element.21) | copy-start | bytes 3932164
  583.7 12.9 %copy-start.4 = (bf16[512,1280]{1,0:T(8,128)(2,1)S(1)}, bf16[512,1280]{1,0:T(8,128)(2,1)}, u32[]{:S(2)}) copy-start(bf16[512,1280]{1,0:T(8,128)(2,1)} %get-tuple-element.19) | copy-start | bytes 3932164
  583.7 12.9 %copy-start.5 = (bf16[512,1280]{1,0:T(8,128)(2,1)S(1)}, bf16[512,1280]{1,0:T(8,128)(2,1)}, u32[]{:S(2)}) copy-start(bf16[512,1280]{1,0:T(8,128)(2,1)} %get-tuple-element.20) | copy-start | bytes 3932164
  596.6 4.7 copy-start.2
  596.7 4.7 copy-start.3
  601.4 11.1 %copy-start = (f32[2,1280]{1,0:T(2,128)S(1)}, f32[2,1280]{1,0:T(2,128)}, u32[]{:S(2)}) copy-start(f32[2,1280]{1,0:T(2,128)} %get-tuple-element.25) | copy-start | bytes 30724

commit v2 on v1

v2 whole, which is shorter than its diff:
```python
import functools
import math

import jax
import jax.numpy as jnp
from jax import lax
from jax.experimental import pallas as pl
from jax.experimental.pallas import tpu as pltpu
from jax.sharding import PartitionSpec as P

MESH = pl.DeviceIdType.MESH
BF = jnp.bfloat16
F32 = jnp.float32
HEAD_DIM = 64
ROWS = 128
RING = 6
CHUNKS = 12
EPS = 1e-6
GELU_C = math.sqrt(2.0 / math.pi)
GELU_A = 0.044715
LOG2E = math.log2(math.e)


def dot_nn(a, b):
    return jnp.dot(a, b, preferred_element_type=F32)


def dot_nt(a, b):
    return lax.dot_general(a, b, (((1,), (1,)), ((), ())), preferred_element_type=F32)


def dot_tn(a, b):
    return lax.dot_general(a, b, (((0,), (0,)), ((), ())), preferred_element_type=F32)


def norm_stats(h_bf):
    h = h_bf.astype(F32)
    inv = lax.rsqrt(jnp.mean(h * h, axis=-1, keepdims=True) + EPS)
    return h, inv


def norm_grad(dn, h_bf, gain):
    h, inv = norm_stats(h_bf)
    hhat = h * inv
    dgain = jnp.sum(dn * hhat, axis=0, keepdims=True)
    dhhat = dn * gain
    corr = jnp.mean(dhhat * hhat, axis=-1, keepdims=True)
    return inv * (dhhat - hhat * corr), dgain


def gelu_parts(u):
    u2 = u * u
    t = jnp.tanh(u * (GELU_C + (GELU_C * GELU_A) * u2))
    return u2, t


def pipeline_kernel(stages, seq, width, x_ref, y_ref, wqkv, wout, wup, wdown, gain_ref,
                    loss_ref, dgain_ref, n1_o, a_o, n2_o, act_o, du_o, dqkv_o, dhm_o, dho_o, wt,
                    ring, hin, hs, hmid, n1, att, n2, qkv, u_buf, act, acc, dho, dhs, dhm, da, du, dqkv, dkvt, bias, loss_in,
                    sb0, sb1, tb0, tb1, pb0, pb1, gb0, gb1,
                    wsem, tsem, xsem, osem, fs, fr, bs, br, ls, lr):
    me = lax.axis_index('stage')
    data = lax.axis_index('data')
    last = stages - 1
    half = stages // 2
    right = lax.rem(me + 1, stages)
    left = lax.rem(me + stages - 1, stages)
    D = width
    CH = D
    LN = 2 * HEAD_DIM
    pairs = D // LN
    pieces = seq // ROWS
    count = float(seq * width)
    sbuf, tbuf, pbuf, gbuf = (sb0, sb1), (tb0, tb1), (pb0, pb1), (gb0, gb1)

    def fetch(kind, j, slot):
        cols = pl.ds(pl.multiple_of(j * CH, CH), CH)
        src = {'q': lambda: wqkv.at[0, :, cols], 'o': lambda: wout.at[0], 'u': lambda: wup.at[0, :, cols], 'd': lambda: wdown.at[0, cols, :]}[kind]()
        pltpu.make_async_copy(src, ring.at[slot], wsem.at[slot]).start()

    def fetch_bwd(idx):
        slot = lax.rem(idx, RING)
        pltpu.make_async_copy(wt.at[idx], ring.at[slot], wsem.at[slot]).start()

    def arrived(slot):
        pltpu.make_async_copy(wout.at[0], ring.at[slot], wsem.at[slot]).wait()

    def put(idx, p, buf, out):
        return pltpu.make_async_copy(buf, out.at[pl.ds(pl.multiple_of(p * ROWS, ROWS), ROWS)], osem.at[idx, p])

    def fwd_copy(p):
        return pltpu.make_async_remote_copy(src_ref=hs.at[p], dst_ref=hin.at[p], send_sem=fs.at[p], recv_sem=fr.at[p],
                                            device_id=(data, right), device_id_type=MESH)

    def bwd_copy(p):
        return pltpu.make_async_remote_copy(src_ref=dhs.at[p], dst_ref=dho.at[p], send_sem=bs.at[p], recv_sem=br.at[p],
                                            device_id=(data, left), device_id_type=MESH)

    def loss_copy():
        return pltpu.make_async_remote_copy(src_ref=loss_in, dst_ref=loss_in, send_sem=ls.at[0], recv_sem=lr.at[0],
                                            device_id=(data, left), device_id_type=MESH)

    def transpose_weights():
        def fetch_any(b):
            slot = lax.rem(b, 3)
            for odd, kind in ((0, 'd'), (1, 'u')):
                @pl.when((b < 8) & (lax.rem(b, 2) == odd))
                def _(kind=kind):
                    fetch(kind, lax.div(b, 2), slot)

            @pl.when(b == 8)
            def _():
                fetch('o', 0, slot)

            @pl.when(b > 8)
            def _():
                fetch('q', b - 9, slot)

        def store(b):
            slot = lax.rem(b, 3)
            return pltpu.make_async_copy(ring.at[slot + 3], wt.at[b], tsem.at[slot])

        fetch_any(0)
        fetch_any(1)

        @pl.loop(0, CHUNKS)
        def _(b):
            slot = lax.rem(b, 3)

            @pl.when(b + 2 < CHUNKS)
            def _():
                fetch_any(b + 2)
            arrived(slot)

            @pl.when(b >= 3)
            def _():
                store(b - 3).wait()

            @pl.loop(0, D // 256)
            def _(r):
                blk = pl.ds(pl.multiple_of(r * 256, 256), 256)
                ring[slot + 3, :, blk] = ring[slot, blk, :].T
            store(b).start()

        @pl.loop(CHUNKS - 3, CHUNKS)
        def _(b):
            store(b).wait()

    def start_fwd():
        for c in range(3):
            fetch('q', c, c)
        fetch('o', 0, 3)
        fetch('u', 0, 4)
        fetch('d', 0, 5)

    @pl.when(me < half)
    def _():
        start_fwd()

    @pl.when(me == 0)
    def _():
        for p in range(pieces):
            pltpu.make_async_copy(x_ref.at[0, pl.ds(p * ROWS, ROWS)], hin.at[p], xsem.at[p]).start()

    @pl.when(me == last)
    def _():
        for p in range(pieces):
            pltpu.make_async_copy(y_ref.at[0, pl.ds(p * ROWS, ROWS)], dho.at[p], xsem.at[p]).start()

    barrier = pltpu.get_barrier_semaphore()
    for nb in (left, right):
        pl.semaphore_signal(barrier, inc=1, device_id=(data, nb), device_id_type=MESH)
    pl.semaphore_wait(barrier, 2)

    @pl.when(me >= half)
    def _():
        transpose_weights()
        start_fwd()

    dgain_ref[...] = jnp.zeros_like(dgain_ref)

    @pl.when(me == last)
    def _():
        loss_in[...] = jnp.zeros_like(loss_in)
    qkv[pl.ds(ROWS, seq - ROWS), pl.ds(D, 2 * D)] = jnp.zeros((seq - ROWS, 2 * D), BF)
    gain0 = gain_ref[0, 0:1, :].astype(F32)
    gain1 = gain_ref[0, 1:2, :].astype(F32)
    low = lax.broadcasted_iota(jnp.int32, (ROWS, LN), 1) < HEAD_DIM

    def stack(a):
        zero = jnp.zeros_like(a)
        return jnp.concatenate([jnp.where(low, a, zero), jnp.where(low, zero, a)], axis=0)

    def unstack(a):
        return jnp.where(low, a[:ROWS], a[ROWS:])

    def lanes(i, base=0):
        return pl.ds(pl.multiple_of(i * LN, LN) + base, LN)

    def set_bias(p):
        r = lax.rem(lax.broadcasted_iota(jnp.int32, (2 * ROWS, seq), 0), ROWS) + p * ROWS
        c = lax.broadcasted_iota(jnp.int32, (2 * ROWS, seq), 1)
        bias[...] = jnp.where(c <= r, 0.0, -1e30)

    def probs(s):
        s = s * (HEAD_DIM ** -0.5 * LOG2E) + bias[...]
        e = jnp.exp2(s - jnp.max(s, axis=-1, keepdims=True))
        return e * (1.0 / jnp.sum(e, axis=-1, keepdims=True))

    def pair_pipeline(first, middle, final):
        first(0, 0)

        @pl.loop(0, pairs // 2)
        def _(h):
            i = 2 * h
            first(i + 1, 1)
            middle(i, 0)
            final(jnp.maximum(i - 1, 0), 1)
            first(jnp.minimum(i + 2, pairs - 1), 0)
            middle(i + 1, 1)
            final(i, 0)
        final(pairs - 1, 1)

    def fwd_piece(p, carry):
        row0 = pl.multiple_of(p * ROWS, ROWS)
        rows = pl.ds(row0, ROWS)
        w = lax.rem(p, 2)
        set_bias(p)

        @pl.when(p >= 2)
        def _():
            put(0, p - 2, n1.at[w], n1_o).wait()
            put(2, p - 2, n2.at[w], n2_o).wait()
            put(3, p - 2, act.at[w], act_o).wait()

        @pl.when(me == 0)
        def _():
            pltpu.make_async_copy(x_ref.at[0, rows], hin.at[p], xsem.at[p]).wait()

        @pl.when(me > 0)
        def _():
            fwd_copy(p).wait_recv()

        def fetch_next(idx, kind, j):
            @pl.when(p < pieces - 1)
            def _():
                fetch(kind, j, idx)

            @pl.when((p == pieces - 1) & (me >= half))
            def _():
                fetch_bwd(idx)

        h, inv = norm_stats(hin[p])
        n1[w] = (h * inv * gain0).astype(BF)
        put(0, p, n1.at[w], n1_o).start()

        @pl.loop(0, 3)
        def _(c):
            arrived(c)
            cols = pl.ds(pl.multiple_of(c * CH, CH), CH)
            qkv[rows, cols] = dot_nn(n1[w], ring[c]).astype(BF)

            @pl.when(c == 0)
            def _():
                fetch('u', 1, 0)

            @pl.when(c == 1)
            def _():
                fetch('d', 1, 1)

            @pl.when(c == 2)
            def _():
                fetch('u', 2, 2)

        def scores(i, b):
            sbuf[b][...] = dot_nt(stack(qkv[rows, lanes(i)]), qkv[:, lanes(i, D)])

        def softmax(i, b):
            pbuf[b][...] = probs(sbuf[b][...]).astype(BF)

        def mix(i, b):
            att[p, :, lanes(i)] = unstack(dot_nn(pbuf[b][...], qkv[:, lanes(i, 2 * D)])).astype(BF)

        pair_pipeline(scores, softmax, mix)

        put(1, p, att.at[p], a_o).start()
        arrived(3)
        hmid[p] = (hin[p].astype(F32) + dot_nn(att[p], ring[3])).astype(BF)
        fetch('d', 2, 3)
        h, inv = norm_stats(hmid[p])
        n2[w] = (h * inv * gain1).astype(BF)
        put(2, p, n2.at[w], n2_o).start()
        acc[...] = hmid[p].astype(F32)

        @pl.loop(0, 4)
        def _(j):
            cols = pl.ds(pl.multiple_of(j * CH, CH), CH)
            s0 = lax.rem(2 * j + 4, RING)
            s1 = s0 + 1
            arrived(s0)
            u_buf[rows, cols] = dot_nn(n2[w], ring[s0])

            @pl.when(j == 0)
            def _():
                fetch('u', 3, 4)

            for jj, kind, jn in ((1, 'q', 0), (2, 'q', 2), (3, 'u', 0)):
                @pl.when(j == jj)
                def _(jj=jj, kind=kind, jn=jn):
                    fetch_next(2 * (jj - 1), kind, jn)
            u = u_buf[rows, cols]
            u2, t = gelu_parts(u)
            act[w, :, cols] = (0.5 * u * (1.0 + t)).astype(BF)
            arrived(s1)
            acc[...] += dot_nn(act[w, :, cols], ring[s1])

            @pl.when(j == 0)
            def _():
                fetch('d', 3, 5)

            for jj, kind, jn in ((1, 'q', 1), (2, 'o', 0), (3, 'd', 0)):
                @pl.when(j == jj)
                def _(jj=jj, kind=kind, jn=jn):
                    fetch_next(2 * (jj - 1) + 1, kind, jn)

        hs[p] = acc[...].astype(BF)

        @pl.when(me < last)
        def _():
            fwd_copy(p).start()

        put(3, p, act.at[w], act_o).start()

        @pl.when(me == last)
        def _():
            pltpu.make_async_copy(y_ref.at[0, rows], dho.at[p], xsem.at[p]).wait()
            err = hs[p].astype(F32) - dho[p].astype(F32)
            dho[p] = (err / count).astype(BF)
            part = jnp.sum(jnp.sum(err * err, axis=0, keepdims=True), axis=1, keepdims=True)
            loss_in[...] += part * (0.5 / count)
        return carry

    lax.fori_loop(0, pieces, fwd_piece, 0)

    @pl.when(me < half)
    def _():
        transpose_weights()
        for b in range(RING):
            fetch_bwd(b)
    dkvt[...] = jnp.zeros_like(dkvt)

    def bwd_piece(t, carry):
        p = pieces - 1 - t
        row0 = pl.multiple_of(p * ROWS, ROWS)
        rows = pl.ds(row0, ROWS)
        w = lax.rem(t, 2)
        set_bias(p)
        for b in range(2):
            pbuf[b][...] = jnp.zeros_like(pbuf[b])
            gbuf[b][...] = jnp.zeros_like(gbuf[b])

        @pl.when(t >= 2)
        def _():
            put(4, p + 2, du.at[w], du_o).wait()
            put(5, p + 2, dqkv.at[w], dqkv_o).wait()
            put(6, p + 2, dhm.at[w], dhm_o).wait()

        @pl.when(me < last)
        def _():
            bwd_copy(p).wait_recv()

        @pl.when((me < last) & (t == 0))
        def _():
            loss_copy().wait_recv()

        @pl.when((me > 0) & (t == 0))
        def _():
            loss_copy().start()
        put(7, p, dho.at[p], dho_o).start()

        def fetch_next(idx):
            nxt = idx + RING

            @pl.when(nxt < CHUNKS)
            def _():
                fetch_bwd(nxt)

            @pl.when((nxt >= CHUNKS) & (t < pieces - 1))
            def _():
                fetch_bwd(nxt - CHUNKS)

        acc[...] = jnp.zeros_like(acc)

        @pl.loop(0, 4)
        def _(j):
            cols = pl.ds(pl.multiple_of(j * CH, CH), CH)
            s0 = lax.rem(2 * j, RING)
            s1 = s0 + 1
            arrived(s0)
            dact = dot_nn(dho[p], ring[s0])
            u = u_buf[rows, cols]
            u2, th = gelu_parts(u)
            slope = 0.5 * (1.0 + th) + (0.5 * u) * (1.0 - th * th) * (GELU_C + (3.0 * GELU_C * GELU_A) * u2)
            du[w, :, cols] = (dact * slope).astype(BF)
            fetch_next(2 * j)
            arrived(s1)
            acc[...] += dot_nn(du[w, :, cols], ring[s1])
            fetch_next(2 * j + 1)

        put(4, p, du.at[w], du_o).start()
        dh, dg = norm_grad(acc[...], hmid[p], gain1)
        dgain_ref[1:2, :] += dg
        dhm[w] = (dho[p].astype(F32) + dh).astype(BF)
        put(6, p, dhm.at[w], dhm_o).start()
        arrived(8 % RING)
        da[...] = dot_nn(dhm[w], ring[8 % RING]).astype(BF)
        fetch_next(8)

        def scores(i, b):
            sbuf[b][...] = dot_nt(stack(qkv[rows, lanes(i)]), qkv[:, lanes(i, D)])
            tbuf[b][...] = dot_nt(stack(da[:, lanes(i)]), qkv[:, lanes(i, 2 * D)])

        def slopes(i, b):
            pr = probs(sbuf[b][...])
            prod = da[:, lanes(i)].astype(F32) * att[p, :, lanes(i)].astype(F32)
            both = jnp.concatenate([jnp.where(low, prod, 0.0), jnp.where(low, 0.0, prod)], axis=0)
            delta = jnp.sum(both, axis=-1, keepdims=True)
            pbuf[b][...] = pr.astype(BF)
            gbuf[b][...] = (pr * (tbuf[b][...] - delta)).astype(BF)

        def grads(i, b):
            scale = HEAD_DIM ** -0.5
            dqkv[w, :, lanes(i)] = (unstack(dot_nn(gbuf[b][...], qkv[:, lanes(i, D)])) * scale).astype(BF)
            dkvt[lanes(i), :] += dot_tn(stack(qkv[rows, lanes(i)]) * scale, gbuf[b][...])
            dkvt[lanes(i, D), :] += dot_tn(stack(da[:, lanes(i)]), pbuf[b][...])

        pair_pipeline(scores, slopes, grads)

        @pl.loop(0, 2 * pairs)
        def _(i):
            dqkv[w, :, lanes(i, D)] = dkvt[lanes(i), rows].T.astype(BF)

        put(5, p, dqkv.at[w], dqkv_o).start()
        acc[...] = jnp.zeros_like(acc)

        @pl.loop(0, 3)
        def _(c):
            slot = c + 9 % RING
            arrived(slot)
            cols = pl.ds(pl.multiple_of(c * CH, CH), CH)
            acc[...] += dot_nn(dqkv[w, :, cols], ring[slot])
            fetch_next(c + 9)

        dh, dg = norm_grad(acc[...], hin[p], gain0)
        dgain_ref[0:1, :] += dg

        @pl.when(me > 0)
        def _():
            dhs[p] = (dhm[w].astype(F32) + dh).astype(BF)
            bwd_copy(p).start()
        return carry

    lax.fori_loop(0, pieces, bwd_piece, 0)
    loss_ref[...] = loss_in[...]

    for p in range(pieces):
        put(1, p, att.at[p], a_o).wait()
        put(7, p, dho.at[p], dho_o).wait()

        @pl.when(me < last)
        def _():
            fwd_copy(p).wait_send()

        @pl.when(me > 0)
        def _():
            bwd_copy(p).wait_send()
    for e in range(2):
        p = pieces - 2 + e
        put(0, p, n1.at[e], n1_o).wait()
        put(2, p, n2.at[e], n2_o).wait()
        put(3, p, act.at[e], act_o).wait()
        put(4, e, du.at[1 - e], du_o).wait()
        put(5, e, dqkv.at[1 - e], dqkv_o).wait()
        put(6, e, dhm.at[1 - e], dhm_o).wait()

    @pl.when(me > 0)
    def _():
        loss_copy().wait_send()


def run_pipeline(stages, x, y, w_qkv, w_out, w_up, w_down, gain):
    seq, width = x.shape[1], x.shape[2]
    ffn = w_up.shape[2]
    pieces = seq // ROWS
    hbm = pl.BlockSpec(memory_space=pl.ANY)
    vmem = pl.BlockSpec(memory_space=pltpu.VMEM)
    V = pltpu.VMEM
    full = V((pieces, ROWS, width), BF)
    two = V((2, ROWS, width), BF)
    wide = V((2 * ROWS, seq), F32)
    tight = V((2 * ROWS, seq), BF)
    widths = (width, width, width, ffn, ffn, 3 * width, width, width)
    outs = [jax.ShapeDtypeStruct((8, 128), F32), jax.ShapeDtypeStruct((2, width), F32)]
    outs += [jax.ShapeDtypeStruct((seq, w), BF) for w in widths]
    outs += [jax.ShapeDtypeStruct((CHUNKS, width, width), BF)]
    dma = pltpu.SemaphoreType.DMA
    return pl.pallas_call(
        functools.partial(pipeline_kernel, stages, seq, width),
        out_shape=outs,
        in_specs=[hbm] * 6 + [vmem],
        out_specs=[vmem, vmem] + [hbm] * 9,
        scratch_shapes=[
            V((RING, width, width), BF),
            full, full, full,
            two, full, two,
            V((seq, 3 * width), BF),
            V((seq, ffn), F32),
            V((2, ROWS, ffn), BF),
            V((ROWS, width), F32),
            full, full, two, V((ROWS, width), BF),
            V((2, ROWS, ffn), BF), V((2, ROWS, 3 * width), BF),
            V((2 * width, seq), F32),
            wide, V((8, 128), F32),
            wide, wide, wide, wide, tight, tight, tight, tight,
            dma((RING,)), dma((3,)), dma((pieces,)), dma((8, pieces)),
            dma((pieces,)), dma((pieces,)), dma((pieces,)), dma((pieces,)), dma((1,)), dma((1,)),
        ],
        compiler_params=pltpu.CompilerParams(collective_id=0, has_side_effects=True, vmem_limit_bytes=67043328),
        name='pipeline',
    )(x, y, w_qkv, w_out, w_up, w_down, gain)


def solution(mesh):
    stages = mesh.shape['stage']

    def per_device(x, y, w_qkv, w_out, w_up, w_down, norm_gain):
        loss, dgain, n1, att, n2, act, du, dqkv, dhm, dho, _ = run_pipeline(stages, x, y, w_qkv, w_out, w_up, w_down, norm_gain)
        g_qkv = dot_tn(n1, dqkv)
        g_out = dot_tn(att, dhm)
        g_up = dot_tn(n2, du)
        g_down = dot_tn(act, dho)
        return loss[0, 0].reshape(1), g_qkv[None], g_out[None], g_up[None], g_down[None], dgain[None]

    weight_spec = P('stage')
    grad_spec = P(('data', 'stage'))
    return jax.shard_map(per_device, mesh=mesh, in_specs=(P('data'), P('data')) + (weight_spec,) * 5,
                         out_specs=(P('data'),) + (grad_spec,) * 5, check_vma=False)
```

time: 613 us -> 403 us (0.66)
  Pallas kernels: 568 us -> 357 us
    pallas_call x1, Pallas kernels: 568 us -> 357 us  [run_pipeline(): pl.pallas_call(functools.partial(pipeline_kernel, stages, seq, width), ou...]
where the time goes in v2:
time: 403 us; the launch traced here: 402 us
  Pallas kernels  357 us (89%)
  matrix products  42.6 us (11%)
    pallas_call x1, Pallas kernels, run_pipeline(): pl.pallas_call(functools.partial(pipeline_kernel, stages, seq, width), ou...  357 us
    dot_general x4, matrix products, dot_tn(): lax.dot_general(a, b, (((0,), (0,)), ((), ())), preferred_element_type=F32)  42.6 us

profile of v2, /device:TPU:0, one launch (start us, length us, event | category | flops | bytes accessed | tf_op | source)
XLA Modules:
  0.0 402.5 jit_solution(17854607027569274886)
XLA Ops:
  0.6 357.3 %pipeline.1 = (f32[8,128]{1,0:T(8,128)}, f32[2,1280]{1,0:T(2,128)}, bf16[512,1280]{1,0:T(8,128)(2,1)}, bf16[512,1280]{1,0:T(8,128)(2,1)}, bf16[512,1280]{1,0:T(8...) custom-call(bf16[1,512,1280]{2,1,0:T(8,128)(2,1)} %x_ref.1, ...), custom_call_target="tpu_custom_call" | custom-call | tf_op jit(solution)/shard_map/pipeline/pallas_call | solution.py:507
  358.0 0.0 copy-start.1
  358.0 0.0 copy-start.6
  358.0 15.1 %convolution_bitcast_fusion = f32[1,5120,1280]{2,1,0:T(8,128)} fusion(bf16[512,5120]{1,0:T(8,128)(2,1)} %get-tuple-element.23, bf16[512,1280]{1,0:T(8,128)(2,1)} %get-tuple-element.24), kind=kOutput, calls=%fused_computation | convolution fusion | flops 6710886400 | bytes 32768000 | tf_op jit(solution)/shard_map/dot_general | solution.py:33
  373.1 0.0 copy-done.1
  373.1 0.0 copy-done.6
  373.1 0.0 copy-start.4
  373.1 0.0 copy-start.5
  373.2 12.9 %convolution_bitcast_fusion.1 = f32[1,1280,5120]{2,1,0:T(8,128)} fusion(bf16[512,1280]{1,0:T(8,128)(2,1)S(1)} %copy-done.6, bf16[512,5120]{1,0:T(8,128)(2,1)S(1)} %copy-done.1), kind=kOutput, calls=%fused_computation.1 | convolution fusion | flops 6710886400 | bytes 32768000 | tf_op jit(solution)/shard_map/dot_general | solution.py:33
  386.1 0.0 copy-done.4
  386.1 0.0 copy-done.5
  386.1 0.0 copy-start.2
  386.1 0.0 copy-start.3
  386.1 4.7 %convolution_bitcast_fusion.3 = f32[1,1280,1280]{2,1,0:T(8,128)} fusion(bf16[512,1280]{1,0:T(8,128)(2,1)S(1)} %copy-done.4, bf16[512,1280]{1,0:T(8,128)(2,1)S(1)} %copy-done.5), kind=kOutput, calls=%fused_computation.3 | convolution fusion | flops 1677721600 | bytes 9175040 | tf_op jit(solution)/shard_map/dot_general | solution.py:33
  390.8 0.0 copy-done.2
  390.8 0.0 copy-done.3
  390.8 0.0 copy-start
  390.8 9.9 %convolution_bitcast_fusion.2 = f32[1,1280,3840]{2,1,0:T(8,128)} fusion(bf16[512,1280]{1,0:T(8,128)(2,1)S(1)} %copy-done.3, bf16[512,3840]{1,0:T(8,128)(2,1)S(1)} %copy-done.2), kind=kOutput, calls=%fused_computation.2 | convolution fusion | flops 5033164800 | bytes 24903680 | tf_op jit(solution)/shard_map/dot_general | solution.py:33
  400.7 1.2 slice.3
  401.9 0.0 copy-done
  401.9 0.6 copy.14
Async XLA Ops:
  358.0 15.2 %copy-start.1 = (bf16[512,5120]{1,0:T(8,128)(2,1)S(1)}, bf16[512,5120]{1,0:T(8,128)(2,1)}, u32[]{:S(2)}) copy-start(bf16[512,5120]{1,0:T(8,128)(2,1)} %get-tuple-element.22) | copy-start | bytes 15728644
  358.0 15.2 %copy-start.6 = (bf16[512,1280]{1,0:T(8,128)(2,1)S(1)}, bf16[512,1280]{1,0:T(8,128)(2,1)}, u32[]{:S(2)}) copy-start(bf16[512,1280]{1,0:T(8,128)(2,1)} %get-tuple-element.21) | copy-start | bytes 3932164
  373.1 12.9 %copy-start.4 = (bf16[512,1280]{1,0:T(8,128)(2,1)S(1)}, bf16[512,1280]{1,0:T(8,128)(2,1)}, u32[]{:S(2)}) copy-start(bf16[512,1280]{1,0:T(8,128)(2,1)} %get-tuple-element.19) | copy-start | bytes 3932164
  373.1 12.9 %copy-start.5 = (bf16[512,1280]{1,0:T(8,128)(2,1)S(1)}, bf16[512,1280]{1,0:T(8,128)(2,1)}, u32[]{:S(2)}) copy-start(bf16[512,1280]{1,0:T(8,128)(2,1)} %get-tuple-element.20) | copy-start | bytes 3932164
  386.1 4.7 %copy-start.2 = (bf16[512,3840]{1,0:T(8,128)(2,1)S(1)}, bf16[512,3840]{1,0:T(8,128)(2,1)}, u32[]{:S(2)}) copy-start(bf16[512,3840]{1,0:T(8,128)(2,1)} %get-tuple-element.18) | copy-start | bytes 11796484
  386.1 4.7 %copy-start.3 = (bf16[512,1280]{1,0:T(8,128)(2,1)S(1)}, bf16[512,1280]{1,0:T(8,128)(2,1)}, u32[]{:S(2)}) copy-start(bf16[512,1280]{1,0:T(8,128)(2,1)} %get-tuple-element.17) | copy-start | bytes 3932164
  390.8 11.1 %copy-start = (f32[2,1280]{1,0:T(2,128)S(1)}, f32[2,1280]{1,0:T(2,128)}, u32[]{:S(2)}) copy-start(f32[2,1280]{1,0:T(2,128)} %get-tuple-element.25) | copy-start | bytes 30724

commit v3 on v2

--- a/solution.py
+++ b/solution.py
@@ -15,6 +15,7 @@
 ROWS = 128
 RING = 6
 CHUNKS = 12
+STAGES = 3
 EPS = 1e-6
 GELU_C = math.sqrt(2.0 / math.pi)
 GELU_A = 0.044715
@@ -56,9 +57,9 @@
 
 def pipeline_kernel(stages, seq, width, x_ref, y_ref, wqkv, wout, wup, wdown, gain_ref,
                     loss_ref, dgain_ref, n1_o, a_o, n2_o, act_o, du_o, dqkv_o, dhm_o, dho_o, wt,
-                    ring, hin, hs, hmid, n1, att, n2, qkv, u_buf, act, acc, dho, dhs, dhm, da, du, dqkv, dkvt, bias, loss_in,
-                    sb0, sb1, tb0, tb1, pb0, pb1, gb0, gb1,
-                    wsem, tsem, xsem, osem, fs, fr, bs, br, ls, lr):
+                    ring, hin, hs, hmid, n1, att, n2, qkv, u_buf, act, acc, dho, bias, loss_in,
+                    sb0, sb1, pb0, pb1,
+                    wsem, esem, tsem, xsem, osem, fs, fr, bs, br, ls, lr):
     me = lax.axis_index('stage')
     data = lax.axis_index('data')
     last = stages - 1
@@ -71,12 +72,15 @@
     pairs = D // LN
     pieces = seq // ROWS
     count = float(seq * width)
-    sbuf, tbuf, pbuf, gbuf = (sb0, sb1), (tb0, tb1), (pb0, pb1), (gb0, gb1)
-
-    def fetch(kind, j, slot):
+    sbuf, pbuf = (sb0, sb1), (pb0, pb1)
+
+    def fetch(kind, j, slot, extra=None):
         cols = pl.ds(pl.multiple_of(j * CH, CH), CH)
         src = {'q': lambda: wqkv.at[0, :, cols], 'o': lambda: wout.at[0], 'u': lambda: wup.at[0, :, cols], 'd': lambda: wdown.at[0, cols, :]}[kind]()
-        pltpu.make_async_copy(src, ring.at[slot], wsem.at[slot]).start()
+        if extra is None:
+            pltpu.make_async_copy(src, ring.at[slot], wsem.at[slot]).start()
+        else:
+            pltpu.make_async_copy(src, extra.at[slot], esem.at[slot]).start()
 
     def fetch_bwd(idx):
         slot = lax.rem(idx, RING)
@@ -93,7 +97,7 @@
                                             device_id=(data, right), device_id_type=MESH)
 
     def bwd_copy(p):
-        return pltpu.make_async_remote_copy(src_ref=dhs.at[p], dst_ref=dho.at[p], send_sem=bs.at[p], recv_sem=br.at[p],
+        return pltpu.make_async_remote_copy(src_ref=hs.at[p], dst_ref=dho.at[p], send_sem=bs.at[p], recv_sem=br.at[p],
                                             device_id=(data, left), device_id_type=MESH)
 
     def loss_copy():
@@ -146,16 +150,14 @@
         def _(b):
             store(b).wait()
 
-    def start_fwd():
+    def start_fwd(extra):
         for c in range(3):
             fetch('q', c, c)
         fetch('o', 0, 3)
         fetch('u', 0, 4)
         fetch('d', 0, 5)
-
-    @pl.when(me < half)
-    def _():
-        start_fwd()
+        for e, (kind, j) in enumerate((('u', 1), ('d', 1), ('u', 2), ('d', 2), ('d', 3))):
+            fetch(kind, j, e, extra)
 
     @pl.when(me == 0)
     def _():
@@ -175,7 +177,6 @@
     @pl.when(me >= half)
     def _():
         transpose_weights()
-        start_fwd()
 
     dgain_ref[...] = jnp.zeros_like(dgain_ref)
 
@@ -221,7 +222,7 @@
             final(i, 0)
         final(pairs - 1, 1)
 
-    def fwd_piece(p, carry):
+    def fwd_piece(extra, p, carry):
         row0 = pl.multiple_of(p * ROWS, ROWS)
         rows = pl.ds(row0, ROWS)
         w = lax.rem(p, 2)
@@ -241,36 +242,24 @@
         def _():
             fwd_copy(p).wait_recv()
 
-        def fetch_next(idx, kind, j):
-            @pl.when(p < pieces - 1)
-            def _():
-                fetch(kind, j, idx)
-
-            @pl.when((p == pieces - 1) & (me >= half))
-            def _():
-                fetch_bwd(idx)
+        @pl.when(p == 0)
+        def _():
+            for c in range(3):
+                arrived(c)
+
+        turn = (p == pieces - 1) & (me >= half)
 
         h, inv = norm_stats(hin[p])
         n1[w] = (h * inv * gain0).astype(BF)
         put(0, p, n1.at[w], n1_o).start()
 
-        @pl.loop(0, 3)
-        def _(c):
-            arrived(c)
-            cols = pl.ds(pl.multiple_of(c * CH, CH), CH)
-            qkv[rows, cols] = dot_nn(n1[w], ring[c]).astype(BF)
-
-            @pl.when(c == 0)
-            def _():
-                fetch('u', 1, 0)
-
-            @pl.when(c == 1)
-            def _():
-                fetch('d', 1, 1)
-
-            @pl.when(c == 2)
-            def _():
-                fetch('u', 2, 2)
+        for c in range(3):
+            qkv[rows, c * CH:(c + 1) * CH] = dot_nn(n1[w], ring[c]).astype(BF)
+
+        @pl.when(turn)
+        def _():
+            for c in range(3):
+                fetch_bwd(c)
 
         def scores(i, b):
             sbuf[b][...] = dot_nt(stack(qkv[rows, lanes(i)]), qkv[:, lanes(i, D)])
@@ -286,50 +275,51 @@
         put(1, p, att.at[p], a_o).start()
         arrived(3)
         hmid[p] = (hin[p].astype(F32) + dot_nn(att[p], ring[3])).astype(BF)
-        fetch('d', 2, 3)
+        fetch('u', 3, 3)
         h, inv = norm_stats(hmid[p])
         n2[w] = (h * inv * gain1).astype(BF)
         put(2, p, n2.at[w], n2_o).start()
-        acc[...] = hmid[p].astype(F32)
-
-        @pl.loop(0, 4)
-        def _(j):
-            cols = pl.ds(pl.multiple_of(j * CH, CH), CH)
-            s0 = lax.rem(2 * j + 4, RING)
-            s1 = s0 + 1
-            arrived(s0)
-            u_buf[rows, cols] = dot_nn(n2[w], ring[s0])
-
-            @pl.when(j == 0)
-            def _():
-                fetch('u', 3, 4)
-
-            for jj, kind, jn in ((1, 'q', 0), (2, 'q', 2), (3, 'u', 0)):
-                @pl.when(j == jj)
-                def _(jj=jj, kind=kind, jn=jn):
-                    fetch_next(2 * (jj - 1), kind, jn)
-            u = u_buf[rows, cols]
+
+        @pl.when(p == 0)
+        def _():
+            arrived(4)
+            arrived(5)
+            for e in range(5):
+                pltpu.make_async_copy(wout.at[0], extra.at[e], esem.at[e]).wait()
+
+        def up(j, weight):
+            u_buf[rows, j * CH:(j + 1) * CH] = dot_nn(n2[w], weight[...])
+
+        def down(j, weight):
+            u = u_buf[rows, j * CH:(j + 1) * CH]
             u2, t = gelu_parts(u)
-            act[w, :, cols] = (0.5 * u * (1.0 + t)).astype(BF)
-            arrived(s1)
-            acc[...] += dot_nn(act[w, :, cols], ring[s1])
-
-            @pl.when(j == 0)
-            def _():
-                fetch('d', 3, 5)
-
-            for jj, kind, jn in ((1, 'q', 1), (2, 'o', 0), (3, 'd', 0)):
-                @pl.when(j == jj)
-                def _(jj=jj, kind=kind, jn=jn):
-                    fetch_next(2 * (jj - 1) + 1, kind, jn)
-
-        hs[p] = acc[...].astype(BF)
+            act[w, :, j * CH:(j + 1) * CH] = (0.5 * u * (1.0 + t)).astype(BF)
+            return dot_nn(act[w, :, j * CH:(j + 1) * CH], weight[...])
+
+        up(0, ring.at[4])
+        up(1, extra.at[0])
+        acc[...] = hmid[p].astype(F32) + down(0, ring.at[5])
+        up(2, extra.at[2])
+        acc[...] += down(1, extra.at[1])
+        arrived(3)
+        up(3, ring.at[3])
+        acc[...] += down(2, extra.at[3])
+        hs[p] = (acc[...] + down(3, extra.at[4])).astype(BF)
 
         @pl.when(me < last)
         def _():
             fwd_copy(p).start()
 
         put(3, p, act.at[w], act_o).start()
+
+        @pl.when(p < pieces - 1)
+        def _():
+            fetch('o', 0, 3)
+
+        @pl.when(turn)
+        def _():
+            for b in range(3, RING):
+                fetch_bwd(b)
 
         @pl.when(me == last)
         def _():
@@ -340,16 +330,19 @@
             loss_in[...] += part * (0.5 / count)
         return carry
 
-    lax.fori_loop(0, pieces, fwd_piece, 0)
+    def forward(extra):
+        start_fwd(extra)
+        lax.fori_loop(0, pieces, functools.partial(fwd_piece, extra), 0)
+
+    pl.run_scoped(forward, pltpu.VMEM((5, D, D), BF))
 
     @pl.when(me < half)
     def _():
         transpose_weights()
         for b in range(RING):
             fetch_bwd(b)
-    dkvt[...] = jnp.zeros_like(dkvt)
-
-    def bwd_piece(t, carry):
+    def bwd_piece(bufs, t, carry):
+        tbuf, gbuf, dbuf, du, dqkv, dhm, da, dkvt = bufs
         p = pieces - 1 - t
         row0 = pl.multiple_of(p * ROWS, ROWS)
         rows = pl.ds(row0, ROWS)
@@ -380,32 +373,39 @@
 
         def fetch_next(idx):
             nxt = idx + RING
-
-            @pl.when(nxt < CHUNKS)
-            def _():
+            if nxt < CHUNKS:
                 fetch_bwd(nxt)
-
-            @pl.when((nxt >= CHUNKS) & (t < pieces - 1))
-            def _():
-                fetch_bwd(nxt - CHUNKS)
-
-        acc[...] = jnp.zeros_like(acc)
-
-        @pl.loop(0, 4)
-        def _(j):
-            cols = pl.ds(pl.multiple_of(j * CH, CH), CH)
-            s0 = lax.rem(2 * j, RING)
-            s1 = s0 + 1
-            arrived(s0)
-            dact = dot_nn(dho[p], ring[s0])
+            else:
+                @pl.when(t < pieces - 1)
+                def _():
+                    fetch_bwd(nxt - CHUNKS)
+
+        def back_down(j):
+            arrived(2 * j % RING)
+            dbuf[j % 2][...] = dot_nn(dho[p], ring[2 * j % RING])
+
+        def back_up(j):
+            cols = slice(j * CH, (j + 1) * CH)
             u = u_buf[rows, cols]
             u2, th = gelu_parts(u)
             slope = 0.5 * (1.0 + th) + (0.5 * u) * (1.0 - th * th) * (GELU_C + (3.0 * GELU_C * GELU_A) * u2)
-            du[w, :, cols] = (dact * slope).astype(BF)
-            fetch_next(2 * j)
-            arrived(s1)
-            acc[...] += dot_nn(du[w, :, cols], ring[s1])
+            du[w, :, cols] = (dbuf[j % 2][...] * slope).astype(BF)
+            return dot_nn(du[w, :, cols], ring[(2 * j + 1) % RING])
+
+        back_down(0)
+        fetch_next(0)
+        for j in range(4):
+            arrived((2 * j + 1) % RING)
+            if j < 3:
+                back_down(j + 1)
+            part = back_up(j)
+            if j == 0:
+                acc[...] = part
+            else:
+                acc[...] += part
             fetch_next(2 * j + 1)
+            if j < 3:
+                fetch_next(2 * j + 2)
 
         put(4, p, du.at[w], du_o).start()
         dh, dg = norm_grad(acc[...], hmid[p], gain1)
@@ -441,33 +441,46 @@
             dqkv[w, :, lanes(i, D)] = dkvt[lanes(i), rows].T.astype(BF)
 
         put(5, p, dqkv.at[w], dqkv_o).start()
-        acc[...] = jnp.zeros_like(acc)
-
-        @pl.loop(0, 3)
-        def _(c):
-            slot = c + 9 % RING
-            arrived(slot)
-            cols = pl.ds(pl.multiple_of(c * CH, CH), CH)
-            acc[...] += dot_nn(dqkv[w, :, cols], ring[slot])
+        for c in range(3):
+            arrived((c + 9) % RING)
+        dn = dot_nn(dqkv[w, :, 0:CH], ring[9 % RING])
+        for c in range(1, 3):
+            dn = dn + dot_nn(dqkv[w, :, c * CH:(c + 1) * CH], ring[(c + 9) % RING])
+        acc[...] = dn
+        for c in range(3):
             fetch_next(c + 9)
-
         dh, dg = norm_grad(acc[...], hin[p], gain0)
         dgain_ref[0:1, :] += dg
 
         @pl.when(me > 0)
         def _():
-            dhs[p] = (dhm[w].astype(F32) + dh).astype(BF)
+            @pl.when(me < last)
+            def _():
+                fwd_copy(p).wait_send()
+            hs[p] = (dhm[w].astype(F32) + dh).astype(BF)
             bwd_copy(p).start()
         return carry
 
-    lax.fori_loop(0, pieces, bwd_piece, 0)
+    def backward(tb0, tb1, gb0, gb1, db0, db1, du, dqkv, dhm, da, dkvt):
+        dkvt[...] = jnp.zeros_like(dkvt)
+        bufs = ((tb0, tb1), (gb0, gb1), (db0, db1), du, dqkv, dhm, da, dkvt)
+        lax.fori_loop(0, pieces, functools.partial(bwd_piece, bufs), 0)
+        for e in range(2):
+            put(4, e, du.at[1 - e], du_o).wait()
+            put(5, e, dqkv.at[1 - e], dqkv_o).wait()
+            put(6, e, dhm.at[1 - e], dhm_o).wait()
+
+    wide, tight, part = pltpu.VMEM((2 * ROWS, seq), F32), pltpu.VMEM((2 * ROWS, seq), BF), pltpu.VMEM((ROWS, D), F32)
+    pl.run_scoped(backward, wide, wide, tight, tight, part, part,
+                  pltpu.VMEM((2, ROWS, 4 * CH), BF), pltpu.VMEM((2, ROWS, 3 * CH), BF), pltpu.VMEM((2, ROWS, D), BF),
+                  pltpu.VMEM((ROWS, D), BF), pltpu.VMEM((2 * D, seq), F32))
     loss_ref[...] = loss_in[...]
 
     for p in range(pieces):
         put(1, p, att.at[p], a_o).wait()
         put(7, p, dho.at[p], dho_o).wait()
 
-        @pl.when(me < last)
+        @pl.when(me == 0)
         def _():
             fwd_copy(p).wait_send()
 
@@ -479,9 +492,6 @@
         put(0, p, n1.at[e], n1_o).wait()
         put(2, p, n2.at[e], n2_o).wait()
         put(3, p, act.at[e], act_o).wait()
-        put(4, e, du.at[1 - e], du_o).wait()
-        put(5, e, dqkv.at[1 - e], dqkv_o).wait()
-        put(6, e, dhm.at[1 - e], dhm_o).wait()
 
     @pl.when(me > 0)
     def _():
@@ -517,12 +527,10 @@
             V((seq, ffn), F32),
             V((2, ROWS, ffn), BF),
             V((ROWS, width), F32),
-            full, full, two, V((ROWS, width), BF),
-            V((2, ROWS, ffn), BF), V((2, ROWS, 3 * width), BF),
-            V((2 * width, seq), F32),
+            full,
             wide, V((8, 128), F32),
-            wide, wide, wide, wide, tight, tight, tight, tight,
-            dma((RING,)), dma((3,)), dma((pieces,)), dma((8, pieces)),
+            wide, wide, tight, tight,
+            dma((RING,)), dma((5,)), dma((3,)), dma((pieces,)), dma((8, pieces)),
             dma((pieces,)), dma((pieces,)), dma((pieces,)), dma((pieces,)), dma((1,)), dma((1,)),
         ],
         compiler_params=pltpu.CompilerParams(collective_id=0, has_side_effects=True, vmem_limit_bytes=67043328),
@@ -530,16 +538,70 @@
     )(x, y, w_qkv, w_out, w_up, w_down, gain)
 
 
+def wgrad_kernel(n1, dqkv, att, dhm, n2, du, act, dho, g_qkv, g_out, g_up, g_down,
+                 n1v, dqkvv, attv, dhmv, n2v, duv, actv, dhov, stage, isem, osem):
+    D = n1.shape[1]
+    T = stage.shape[2]
+    loads = ((att, attv), (dhm, dhmv), (dho, dhov), (act, actv), (n2, n2v), (du, duv), (n1, n1v), (dqkv, dqkvv))
+    copies = [pltpu.make_async_copy(src, dst, isem.at[i]) for i, (src, dst) in enumerate(loads)]
+    for c in copies:
+        c.start()
+
+    def tile(g, r, c):
+        return g.at[0, pl.ds(pl.multiple_of(r * D, D), D), pl.ds(pl.multiple_of(c * T, T), T)]
+
+    def section(base, left, right, g, rows, cols):
+        def step(i, carry):
+            slot = lax.rem(base + i, STAGES)
+            r, c = lax.div(i, cols), lax.rem(i, cols)
+
+            @pl.when(base + i >= STAGES)
+            def _():
+                pltpu.make_async_copy(stage.at[slot], tile(g_out, 0, 0), osem.at[slot]).wait()
+            a = left[:, pl.ds(pl.multiple_of(r * D, D), D)]
+            stage[slot] = dot_tn(a, right[:, pl.ds(pl.multiple_of(c * T, T), T)])
+            pltpu.make_async_copy(stage.at[slot], tile(g, r, c), osem.at[slot]).start()
+            return carry
+        lax.fori_loop(0, rows * cols, step, 0)
+        return base + rows * cols
+
+    base = 0
+    for pair, left, right, g in ((0, attv, dhmv, g_out), (2, actv, dhov, g_down), (4, n2v, duv, g_up), (6, n1v, dqkvv, g_qkv)):
+        if pair != 2:
+            copies[pair].wait()
+            copies[pair + 1].wait()
+        else:
+            copies[2].wait()
+            copies[3].wait()
+        base = section(base, left, right, g, left.shape[1] // D, right.shape[1] // T)
+    for slot in range(STAGES):
+        pltpu.make_async_copy(stage.at[slot], tile(g_out, 0, 0), osem.at[slot]).wait()
+
+
+def weight_grads(n1, dqkv, att, dhm, n2, du, act, dho):
+    D = n1.shape[1]
+    hbm = pl.BlockSpec(memory_space=pl.ANY)
+    ins = (n1, dqkv, att, dhm, n2, du, act, dho)
+    shapes = ((D, dqkv.shape[1]), (D, D), (D, du.shape[1]), (act.shape[1], D))
+    dma = pltpu.SemaphoreType.DMA
+    return pl.pallas_call(
+        wgrad_kernel,
+        out_shape=[jax.ShapeDtypeStruct((1,) + sh, F32) for sh in shapes],
+        in_specs=[hbm] * 8,
+        out_specs=[hbm] * 4,
+        scratch_shapes=[pltpu.VMEM(a.shape, BF) for a in ins] + [pltpu.VMEM((STAGES, D, D // 2), F32), dma((8,)), dma((STAGES,))],
+        compiler_params=pltpu.CompilerParams(vmem_limit_bytes=60 * 2 ** 20),
+        name='weight_grads',
+    )(*ins)
+
+
 def solution(mesh):
     stages = mesh.shape['stage']
 
     def per_device(x, y, w_qkv, w_out, w_up, w_down, norm_gain):
         loss, dgain, n1, att, n2, act, du, dqkv, dhm, dho, _ = run_pipeline(stages, x, y, w_qkv, w_out, w_up, w_down, norm_gain)
-        g_qkv = dot_tn(n1, dqkv)
-        g_out = dot_tn(att, dhm)
-        g_up = dot_tn(n2, du)
-        g_down = dot_tn(act, dho)
-        return loss[0, 0].reshape(1), g_qkv[None], g_out[None], g_up[None], g_down[None], dgain[None]
+        g_qkv, g_out, g_up, g_down = weight_grads(n1, dqkv, att, dhm, n2, du, act, dho)
+        return loss[0, 0].reshape(1), g_qkv, g_out, g_up, g_down, dgain[None]
 
     weight_spec = P('stage')
     grad_spec = P(('data', 'stage'))

time: 403 us -> 370 us (0.918)
  matrix products: 42.6 us -> 0 us
  Pallas kernels: 357 us -> 368 us
    dot_general x4 -> x0, matrix products: 42.6 us -> none  [dot_tn(): lax.dot_general(a, b, (((0,), (0,)), ((), ())), preferred_element_type=F32)]
    pallas_call x0 -> x1, Pallas kernels: none -> 34.2 us  [weight_grads(): pl.pallas_call(wgrad_kernel, out_shape=[jax.ShapeDtypeStruct((1,) + sh, F...]
    pallas_call x1, Pallas kernels: 357 us -> 334 us  [run_pipeline(): pl.pallas_call(functools.partial(pipeline_kernel, stages, seq, width), ou...]
where the time goes in v3:
time: 370 us
  Pallas kernels  368 us (99%)
    pallas_call x1, Pallas kernels, run_pipeline(): pl.pallas_call(functools.partial(pipeline_kernel, stages, seq, width), ou...  334 us
    pallas_call x1, Pallas kernels, weight_grads(): pl.pallas_call(wgrad_kernel, out_shape=[jax.ShapeDtypeStruct((1,) + sh, F...  34.2 us

profile of v3, /device:TPU:0, one launch (start us, length us, event | category | flops | bytes accessed | tf_op | source)
XLA Modules:
  0.0 370.3 jit_solution(11709993108481758983)
XLA Ops:
  0.6 333.6 %pipeline.1 = (f32[8,128]{1,0:T(8,128)}, f32[2,1280]{1,0:T(2,128)}, bf16[512,1280]{1,0:T(8,128)(2,1)}, bf16[512,1280]{1,0:T(8,128)(2,1)}, bf16[512,1280]{1,0:T(8...) custom-call(bf16[1,512,1280]{2,1,0:T(8,128)(2,1)} %x_ref.1, ...), custom_call_target="tpu_custom_call" | custom-call | tf_op jit(solution)/shard_map/pipeline/pallas_call | solution.py:517
  334.3 1.2 slice.3
  335.5 0.0 copy-start
  335.5 34.2 %weight_grads.1 = (f32[1,1280,3840]{2,1,0:T(8,128)}, f32[1,1280,1280]{2,1,0:T(8,128)}, f32[1,1280,5120]{2,1,0:T(8,128)}, f32[1,5120,1280]{2,1,0:T(8,128)}) custom-call(bf16[512,1280]{1,0:T(8,128)(2,1)} %get-tuple-element.21.n1, bf16[512,3840]{1,0:T(8,128)(2,1)} %get-tuple-element.22.dqkv, bf16[512,1280]{1,0:T(8,128)(2,1)} %get-tuple-element.23.att, ...), custom_call_target="tpu_custom_call" | custom-call | tf_op jit(solution)/shard_map/weight_grads/pallas_call | solution.py:587
  369.7 0.0 copy-done
  369.7 0.6 copy.14
Async XLA Ops:
  335.5 34.2 %copy-start = (f32[2,1280]{1,0:T(2,128)S(1)}, f32[2,1280]{1,0:T(2,128)}, u32[]{:S(2)}) copy-start(f32[2,1280]{1,0:T(2,128)} %get-tuple-element.33) | copy-start | bytes 30724

commit v4 on v3

--- a/solution.py
+++ b/solution.py
@@ -58,7 +58,7 @@
 def pipeline_kernel(stages, seq, width, x_ref, y_ref, wqkv, wout, wup, wdown, gain_ref,
                     loss_ref, dgain_ref, n1_o, a_o, n2_o, act_o, du_o, dqkv_o, dhm_o, dho_o, wt,
                     ring, hin, hs, hmid, n1, att, n2, qkv, u_buf, act, acc, dho, bias, loss_in,
-                    sb0, sb1, pb0, pb1,
+                    sb0, sb1, pb0, pb1, lse,
                     wsem, esem, tsem, xsem, osem, fs, fr, bs, br, ls, lr):
     me = lax.axis_index('stage')
     data = lax.axis_index('data')
@@ -183,7 +183,6 @@
     @pl.when(me == last)
     def _():
         loss_in[...] = jnp.zeros_like(loss_in)
-    qkv[pl.ds(ROWS, seq - ROWS), pl.ds(D, 2 * D)] = jnp.zeros((seq - ROWS, 2 * D), BF)
     gain0 = gain_ref[0, 0:1, :].astype(F32)
     gain1 = gain_ref[0, 1:2, :].astype(F32)
     low = lax.broadcasted_iota(jnp.int32, (ROWS, LN), 1) < HEAD_DIM
@@ -198,15 +197,24 @@
     def lanes(i, base=0):
         return pl.ds(pl.multiple_of(i * LN, LN) + base, LN)
 
-    def set_bias(p):
-        r = lax.rem(lax.broadcasted_iota(jnp.int32, (2 * ROWS, seq), 0), ROWS) + p * ROWS
-        c = lax.broadcasted_iota(jnp.int32, (2 * ROWS, seq), 1)
-        bias[...] = jnp.where(c <= r, 0.0, -1e30)
-
-    def probs(s):
-        s = s * (HEAD_DIM ** -0.5 * LOG2E) + bias[...]
-        e = jnp.exp2(s - jnp.max(s, axis=-1, keepdims=True))
-        return e * (1.0 / jnp.sum(e, axis=-1, keepdims=True))
+    r = lax.rem(lax.broadcasted_iota(jnp.int32, (2 * ROWS, ROWS), 0), ROWS)
+    c = lax.broadcasted_iota(jnp.int32, (2 * ROWS, ROWS), 1)
+    bias[...] = jnp.where(c <= r, 0.0, -1e30)
+
+    lane = lax.broadcasted_iota(jnp.int32, (2 * ROWS, 128), 1)
+
+    def masked(s):
+        s = s * (HEAD_DIM ** -0.5 * LOG2E)
+        keys = s.shape[1]
+        if keys > ROWS:
+            return jnp.concatenate([s[:, :keys - ROWS], s[:, keys - ROWS:] + bias[...]], axis=1)
+        return s + bias[...]
+
+    def by_piece(p, body):
+        for k in range(pieces):
+            @pl.when(p == k)
+            def _(k=k):
+                body((k + 1) * ROWS)
 
     def pair_pipeline(first, middle, final):
         first(0, 0)
@@ -226,7 +234,6 @@
         row0 = pl.multiple_of(p * ROWS, ROWS)
         rows = pl.ds(row0, ROWS)
         w = lax.rem(p, 2)
-        set_bias(p)
 
         @pl.when(p >= 2)
         def _():
@@ -261,17 +268,24 @@
             for c in range(3):
                 fetch_bwd(c)
 
-        def scores(i, b):
-            sbuf[b][...] = dot_nt(stack(qkv[rows, lanes(i)]), qkv[:, lanes(i, D)])
-
-        def softmax(i, b):
-            pbuf[b][...] = probs(sbuf[b][...]).astype(BF)
-
-        def mix(i, b):
-            att[p, :, lanes(i)] = unstack(dot_nn(pbuf[b][...], qkv[:, lanes(i, 2 * D)])).astype(BF)
-
-        pair_pipeline(scores, softmax, mix)
-
+        def attend(keys):
+            def scores(i, b):
+                sbuf[b][:, :keys] = dot_nt(stack(qkv[rows, lanes(i)]), qkv[:keys, lanes(i, D)])
+
+            def softmax(i, b):
+                s = masked(sbuf[b][:, :keys])
+                top = jnp.max(s, axis=-1, keepdims=True)
+                e = jnp.exp2(s - top)
+                total = jnp.sum(e, axis=-1, keepdims=True)
+                lse[p] = jnp.where(lane == i, top + jnp.log2(total), lse[p])
+                pbuf[b][:, :keys] = (e * (1.0 / total)).astype(BF)
+
+            def mix(i, b):
+                att[p, :, lanes(i)] = unstack(dot_nn(pbuf[b][:, :keys], qkv[:keys, lanes(i, 2 * D)])).astype(BF)
+
+            pair_pipeline(scores, softmax, mix)
+
+        by_piece(p, attend)
         put(1, p, att.at[p], a_o).start()
         arrived(3)
         hmid[p] = (hin[p].astype(F32) + dot_nn(att[p], ring[3])).astype(BF)
@@ -342,15 +356,11 @@
         for b in range(RING):
             fetch_bwd(b)
     def bwd_piece(bufs, t, carry):
-        tbuf, gbuf, dbuf, du, dqkv, dhm, da, dkvt = bufs
+        gbuf, dbuf, du, dqkv, dhm, da, dkvt = bufs
         p = pieces - 1 - t
         row0 = pl.multiple_of(p * ROWS, ROWS)
         rows = pl.ds(row0, ROWS)
         w = lax.rem(t, 2)
-        set_bias(p)
-        for b in range(2):
-            pbuf[b][...] = jnp.zeros_like(pbuf[b])
-            gbuf[b][...] = jnp.zeros_like(gbuf[b])
 
         @pl.when(t >= 2)
         def _():
@@ -416,25 +426,35 @@
         da[...] = dot_nn(dhm[w], ring[8 % RING]).astype(BF)
         fetch_next(8)
 
-        def scores(i, b):
-            sbuf[b][...] = dot_nt(stack(qkv[rows, lanes(i)]), qkv[:, lanes(i, D)])
-            tbuf[b][...] = dot_nt(stack(da[:, lanes(i)]), qkv[:, lanes(i, 2 * D)])
-
-        def slopes(i, b):
-            pr = probs(sbuf[b][...])
-            prod = da[:, lanes(i)].astype(F32) * att[p, :, lanes(i)].astype(F32)
-            both = jnp.concatenate([jnp.where(low, prod, 0.0), jnp.where(low, 0.0, prod)], axis=0)
-            delta = jnp.sum(both, axis=-1, keepdims=True)
-            pbuf[b][...] = pr.astype(BF)
-            gbuf[b][...] = (pr * (tbuf[b][...] - delta)).astype(BF)
-
-        def grads(i, b):
+        def attend(keys):
             scale = HEAD_DIM ** -0.5
-            dqkv[w, :, lanes(i)] = (unstack(dot_nn(gbuf[b][...], qkv[:, lanes(i, D)])) * scale).astype(BF)
-            dkvt[lanes(i), :] += dot_tn(stack(qkv[rows, lanes(i)]) * scale, gbuf[b][...])
-            dkvt[lanes(i, D), :] += dot_tn(stack(da[:, lanes(i)]), pbuf[b][...])
-
-        pair_pipeline(scores, slopes, grads)
+
+            def slopes(i, b):
+                prod = da[:, lanes(i)].astype(F32) * att[p, :, lanes(i)].astype(F32)
+                both = jnp.concatenate([jnp.where(low, prod, 0.0), jnp.where(low, 0.0, prod)], axis=0)
+                delta = jnp.sum(both, axis=-1, keepdims=True)
+                norm = jnp.sum(jnp.where(lane == i, lse[p], 0.0), axis=-1, keepdims=True)
+                pr = jnp.exp2(masked(dot_nt(stack(qkv[rows, lanes(i)]), qkv[:keys, lanes(i, D)])) - norm)
+                pbuf[b][:, :keys] = pr.astype(BF)
+                dp = dot_nt(stack(da[:, lanes(i)]), qkv[:keys, lanes(i, 2 * D)])
+                gbuf[b][:, :keys] = (pr * (dp - delta)).astype(BF)
+
+            def grads(i, b):
+                g = gbuf[b][:, :keys]
+                dqkv[w, :, lanes(i)] = (unstack(dot_nn(g, qkv[:keys, lanes(i, D)])) * scale).astype(BF)
+                dkvt[lanes(i), :keys] += dot_tn(stack(qkv[rows, lanes(i)]) * scale, g)
+                dkvt[lanes(i, D), :keys] += dot_tn(stack(da[:, lanes(i)]), pbuf[b][:, :keys])
+
+            slopes(0, 0)
+
+            @pl.loop(0, pairs // 2)
+            def _(h):
+                slopes(2 * h + 1, 1)
+                grads(2 * h, 0)
+                slopes(jnp.minimum(2 * h + 2, pairs - 1), 0)
+                grads(2 * h + 1, 1)
+
+        by_piece(p, attend)
 
         @pl.loop(0, 2 * pairs)
         def _(i):
@@ -461,17 +481,17 @@
             bwd_copy(p).start()
         return carry
 
-    def backward(tb0, tb1, gb0, gb1, db0, db1, du, dqkv, dhm, da, dkvt):
+    def backward(gb0, gb1, db0, db1, du, dqkv, dhm, da, dkvt):
         dkvt[...] = jnp.zeros_like(dkvt)
-        bufs = ((tb0, tb1), (gb0, gb1), (db0, db1), du, dqkv, dhm, da, dkvt)
+        bufs = ((gb0, gb1), (db0, db1), du, dqkv, dhm, da, dkvt)
         lax.fori_loop(0, pieces, functools.partial(bwd_piece, bufs), 0)
         for e in range(2):
             put(4, e, du.at[1 - e], du_o).wait()
             put(5, e, dqkv.at[1 - e], dqkv_o).wait()
             put(6, e, dhm.at[1 - e], dhm_o).wait()
 
-    wide, tight, part = pltpu.VMEM((2 * ROWS, seq), F32), pltpu.VMEM((2 * ROWS, seq), BF), pltpu.VMEM((ROWS, D), F32)
-    pl.run_scoped(backward, wide, wide, tight, tight, part, part,
+    tight, part = pltpu.VMEM((2 * ROWS, seq), BF), pltpu.VMEM((ROWS, D), F32)
+    pl.run_scoped(backward, tight, tight, part, part,
                   pltpu.VMEM((2, ROWS, 4 * CH), BF), pltpu.VMEM((2, ROWS, 3 * CH), BF), pltpu.VMEM((2, ROWS, D), BF),
                   pltpu.VMEM((ROWS, D), BF), pltpu.VMEM((2 * D, seq), F32))
     loss_ref[...] = loss_in[...]
@@ -528,8 +548,8 @@
             V((2, ROWS, ffn), BF),
             V((ROWS, width), F32),
             full,
-            wide, V((8, 128), F32),
-            wide, wide, tight, tight,
+            V((2 * ROWS, ROWS), F32), V((8, 128), F32),
+            wide, wide, tight, tight, V((pieces, 2 * ROWS, 128), F32),
             dma((RING,)), dma((5,)), dma((3,)), dma((pieces,)), dma((8, pieces)),
             dma((pieces,)), dma((pieces,)), dma((pieces,)), dma((pieces,)), dma((1,)), dma((1,)),
         ],
@@ -538,13 +558,17 @@
     )(x, y, w_qkv, w_out, w_up, w_down, gain)
 
 
-def wgrad_kernel(n1, dqkv, att, dhm, n2, du, act, dho, g_qkv, g_out, g_up, g_down,
-                 n1v, dqkvv, attv, dhmv, n2v, duv, actv, dhov, stage, isem, osem):
+def wgrad_kernel(n1, dqkv, att, dhm, n2, du, act, dho, loss, dgain, g_qkv, g_out, g_up, g_down, g_gain, loss_out,
+                 n1v, dqkvv, attv, dhmv, n2v, duv, actv, dhov, stage, dgv, lossv, isem, osem, ssem):
     D = n1.shape[1]
     T = stage.shape[2]
     loads = ((att, attv), (dhm, dhmv), (dho, dhov), (act, actv), (n2, n2v), (du, duv), (n1, n1v), (dqkv, dqkvv))
     copies = [pltpu.make_async_copy(src, dst, isem.at[i]) for i, (src, dst) in enumerate(loads)]
     for c in copies:
+        c.start()
+    small_in = [pltpu.make_async_copy(src, dst, ssem.at[i]) for i, (src, dst) in enumerate(((dgain, dgv), (loss.at[0:1], lossv)))]
+    small_out = [pltpu.make_async_copy(src, dst, ssem.at[2 + i]) for i, (src, dst) in enumerate(((dgv, g_gain.at[0]), (lossv, loss_out)))]
+    for c in small_in:
         c.start()
 
     def tile(g, r, c):
@@ -574,11 +598,16 @@
             copies[2].wait()
             copies[3].wait()
         base = section(base, left, right, g, left.shape[1] // D, right.shape[1] // T)
+    for a, b in zip(small_in, small_out):
+        a.wait()
+        b.start()
+    for b in small_out:
+        b.wait()
     for slot in range(STAGES):
         pltpu.make_async_copy(stage.at[slot], tile(g_out, 0, 0), osem.at[slot]).wait()
 
 
-def weight_grads(n1, dqkv, att, dhm, n2, du, act, dho):
+def weight_grads(n1, dqkv, att, dhm, n2, du, act, dho, loss, dgain):
     D = n1.shape[1]
     hbm = pl.BlockSpec(memory_space=pl.ANY)
     ins = (n1, dqkv, att, dhm, n2, du, act, dho)
@@ -586,13 +615,14 @@
     dma = pltpu.SemaphoreType.DMA
     return pl.pallas_call(
         wgrad_kernel,
-        out_shape=[jax.ShapeDtypeStruct((1,) + sh, F32) for sh in shapes],
-        in_specs=[hbm] * 8,
-        out_specs=[hbm] * 4,
-        scratch_shapes=[pltpu.VMEM(a.shape, BF) for a in ins] + [pltpu.VMEM((STAGES, D, D // 2), F32), dma((8,)), dma((STAGES,))],
+        out_shape=[jax.ShapeDtypeStruct((1,) + sh, F32) for sh in shapes + (dgain.shape,)] + [jax.ShapeDtypeStruct((1, 128), F32)],
+        in_specs=[hbm] * 10,
+        out_specs=[hbm] * 6,
+        scratch_shapes=[pltpu.VMEM(a.shape, BF) for a in ins] + [pltpu.VMEM((STAGES, D, D // 2), F32), pltpu.VMEM(dgain.shape, F32), pltpu.VMEM((1, 128), F32),
+                                                                dma((8,)), dma((STAGES,)), dma((4,))],
         compiler_params=pltpu.CompilerParams(vmem_limit_bytes=60 * 2 ** 20),
         name='weight_grads',
-    )(*ins)
+    )(*ins, loss, dgain)
 
 
 def solution(mesh):
@@ -600,8 +630,8 @@
 
     def per_device(x, y, w_qkv, w_out, w_up, w_down, norm_gain):
         loss, dgain, n1, att, n2, act, du, dqkv, dhm, dho, _ = run_pipeline(stages, x, y, w_qkv, w_out, w_up, w_down, norm_gain)
-        g_qkv, g_out, g_up, g_down = weight_grads(n1, dqkv, att, dhm, n2, du, act, dho)
-        return loss[0, 0].reshape(1), g_qkv, g_out, g_up, g_down, dgain[None]
+        g_qkv, g_out, g_up, g_down, g_gain, loss = weight_grads(n1, dqkv, att, dhm, n2, du, act, dho, loss, dgain)
+        return loss[0, :1], g_qkv, g_out, g_up, g_down, g_gain
 
     weight_spec = P('stage')
     grad_spec = P(('data', 'stage'))

time: 370 us -> 349 us (0.943)
  Pallas kernels: 368 us -> 348 us
    pallas_call x1, Pallas kernels: 334 us -> 313 us  [run_pipeline(): pl.pallas_call(functools.partial(pipeline_kernel, stages, seq, width), ou...]
where the time goes in v4:
time: 349 us; the launch traced here: 348 us
  Pallas kernels  348 us (100%)
    pallas_call x1, Pallas kernels, run_pipeline(): pl.pallas_call(functools.partial(pipeline_kernel, stages, seq, width), ou...  313 us
    pallas_call x1, Pallas kernels, weight_grads(): pl.pallas_call(wgrad_kernel, out_shape=[jax.ShapeDtypeStruct((1,) + sh, F...  34.2 us

profile of v4, /device:TPU:0, one launch (start us, length us, event | category | flops | bytes accessed | tf_op | source)
XLA Modules:
  0.0 348.4 jit_solution(5224947024410757392)
XLA Ops:
  0.6 313.4 %pipeline.1 = (f32[8,128]{1,0:T(8,128)}, f32[2,1280]{1,0:T(2,128)}, bf16[512,1280]{1,0:T(8,128)(2,1)}, bf16[512,1280]{1,0:T(8,128)(2,1)}, bf16[512,1280]{1,0:T(8...) custom-call(bf16[1,512,1280]{2,1,0:T(8,128)(2,1)} %x_ref.1, ...), custom_call_target="tpu_custom_call" | custom-call | tf_op jit(solution)/shard_map/pipeline/pallas_call | solution.py:537
  314.0 34.2 %weight_grads.1 = (f32[1,1280,3840]{2,1,0:T(8,128)}, f32[1,1280,1280]{2,1,0:T(8,128)}, f32[1,1280,5120]{2,1,0:T(8,128)}, f32[1,5120,1280]{2,1,0:T(8,128)}, f32[1,2,1280]{2,1,0:T(2,128)}, /*index=5*/f32[1,128]{1,0:T(1,128)}) custom-call(bf16[512,1280]{1,0:T(8,128)(2,1)} %get-tuple-element.22.n1, bf16[512,3840]{1,0:T(8,128)(2,1)} %get-tuple-element.23.dqkv, ...), custom_call_target="tpu_custom_call" | custom-call | tf_op jit(solution)/shard_map/weight_grads/pallas_call | solution.py:616

commit v5 on v4

--- a/solution.py
+++ b/solution.py
@@ -15,7 +15,7 @@
 ROWS = 128
 RING = 6
 CHUNKS = 12
-STAGES = 3
+STAGES = 5
 EPS = 1e-6
 GELU_C = math.sqrt(2.0 / math.pi)
 GELU_A = 0.044715
@@ -391,7 +391,6 @@
                     fetch_bwd(nxt - CHUNKS)
 
         def back_down(j):
-            arrived(2 * j % RING)
             dbuf[j % 2][...] = dot_nn(dho[p], ring[2 * j % RING])
 
         def back_up(j):
@@ -402,20 +401,26 @@
             du[w, :, cols] = (dbuf[j % 2][...] * slope).astype(BF)
             return dot_nn(du[w, :, cols], ring[(2 * j + 1) % RING])
 
+        for idx in range(3):
+            arrived(idx)
         back_down(0)
-        fetch_next(0)
-        for j in range(4):
-            arrived((2 * j + 1) % RING)
-            if j < 3:
-                back_down(j + 1)
-            part = back_up(j)
-            if j == 0:
-                acc[...] = part
-            else:
-                acc[...] += part
-            fetch_next(2 * j + 1)
-            if j < 3:
-                fetch_next(2 * j + 2)
+        back_down(1)
+        acc[...] = back_up(0)
+        for idx in range(3):
+            fetch_next(idx)
+        for idx in range(3, 6):
+            arrived(idx)
+        back_down(2)
+        acc[...] += back_up(1)
+        acc[...] += back_up(2)
+        for idx in range(3, 6):
+            fetch_next(idx)
+        for idx in range(6, 8):
+            arrived(idx % RING)
+        back_down(3)
+        acc[...] += back_up(3)
+        for idx in range(6, 8):
+            fetch_next(idx)
 
         put(4, p, du.at[w], du_o).start()
         dh, dg = norm_grad(acc[...], hmid[p], gain1)
@@ -442,8 +447,14 @@
             def grads(i, b):
                 g = gbuf[b][:, :keys]
                 dqkv[w, :, lanes(i)] = (unstack(dot_nn(g, qkv[:keys, lanes(i, D)])) * scale).astype(BF)
-                dkvt[lanes(i), :keys] += dot_tn(stack(qkv[rows, lanes(i)]) * scale, g)
-                dkvt[lanes(i, D), :keys] += dot_tn(stack(da[:, lanes(i)]), pbuf[b][:, :keys])
+                dk = dot_tn(stack(qkv[rows, lanes(i)]) * scale, g)
+                dv = dot_tn(stack(da[:, lanes(i)]), pbuf[b][:, :keys])
+                if keys == seq:
+                    dkvt[lanes(i), :] = dk
+                    dkvt[lanes(i, D), :] = dv
+                else:
+                    dkvt[lanes(i), :keys] += dk
+                    dkvt[lanes(i, D), :keys] += dv
 
             slopes(0, 0)
 
@@ -456,9 +467,11 @@
 
         by_piece(p, attend)
 
-        @pl.loop(0, 2 * pairs)
-        def _(i):
-            dqkv[w, :, lanes(i, D)] = dkvt[lanes(i), rows].T.astype(BF)
+        @pl.loop(0, 2)
+        def _(g):
+            for e in range(pairs):
+                i = g * pairs + e
+                dqkv[w, :, lanes(i, D)] = dkvt[lanes(i), rows].astype(BF).T
 
         put(5, p, dqkv.at[w], dqkv_o).start()
         for c in range(3):
@@ -482,7 +495,6 @@
         return carry
 
     def backward(gb0, gb1, db0, db1, du, dqkv, dhm, da, dkvt):
-        dkvt[...] = jnp.zeros_like(dkvt)
         bufs = ((gb0, gb1), (db0, db1), du, dqkv, dhm, da, dkvt)
         lax.fori_loop(0, pieces, functools.partial(bwd_piece, bufs), 0)
         for e in range(2):

time: 349 us -> 335 us (0.960)
  Pallas kernels: 348 us -> 334 us
    pallas_call x1, Pallas kernels: 313 us -> 301 us  [run_pipeline(): pl.pallas_call(functools.partial(pipeline_kernel, stages, seq, width), ou...]
where the time goes in v5:
time: 335 us
  Pallas kernels  334 us (100%)
    pallas_call x1, Pallas kernels, run_pipeline(): pl.pallas_call(functools.partial(pipeline_kernel, stages, seq, width), ou...  301 us
    pallas_call x1, Pallas kernels, weight_grads(): pl.pallas_call(wgrad_kernel, out_shape=[jax.ShapeDtypeStruct((1,) + sh, F...  33.5 us

profile of v5, /device:TPU:0, one launch (start us, length us, event | category | flops | bytes accessed | tf_op | source)
XLA Modules:
  0.0 335.3 jit_solution(7523304307848223872)
XLA Ops:
  0.6 301.0 %pipeline.1 = (f32[8,128]{1,0:T(8,128)}, f32[2,1280]{1,0:T(2,128)}, bf16[512,1280]{1,0:T(8,128)(2,1)}, bf16[512,1280]{1,0:T(8,128)(2,1)}, bf16[512,1280]{1,0:T(8...) custom-call(bf16[1,512,1280]{2,1,0:T(8,128)(2,1)} %x_ref.1, ...), custom_call_target="tpu_custom_call" | custom-call | tf_op jit(solution)/shard_map/pipeline/pallas_call | solution.py:549
  301.7 33.5 %weight_grads.1 = (f32[1,1280,3840]{2,1,0:T(8,128)}, f32[1,1280,1280]{2,1,0:T(8,128)}, f32[1,1280,5120]{2,1,0:T(8,128)}, f32[1,5120,1280]{2,1,0:T(8,128)}, f32[1,2,1280]{2,1,0:T(2,128)}, /*index=5*/f32[1,128]{1,0:T(1,128)}) custom-call(bf16[512,1280]{1,0:T(8,128)(2,1)} %get-tuple-element.22.n1, bf16[512,3840]{1,0:T(8,128)(2,1)} %get-tuple-element.23.dqkv, ...), custom_call_target="tpu_custom_call" | custom-call | tf_op jit(solution)/shard_map/weight_grads/pallas_call | solution.py:628

commit v6 on v5

--- a/solution.py
+++ b/solution.py
@@ -195,6 +195,8 @@
         return jnp.where(low, a[:ROWS], a[ROWS:])
 
     def lanes(i, base=0):
+        if isinstance(i, int):
+            return pl.ds(i * LN + base, LN)
         return pl.ds(pl.multiple_of(i * LN, LN) + base, LN)
 
     r = lax.rem(lax.broadcasted_iota(jnp.int32, (2 * ROWS, ROWS), 0), ROWS)
@@ -216,8 +218,17 @@
             def _(k=k):
                 body((k + 1) * ROWS)
 
-    def pair_pipeline(first, middle, final):
+    def pair_pipeline(unrolled, first, middle, final):
         first(0, 0)
+        if unrolled:
+            for i in range(pairs):
+                if i + 1 < pairs:
+                    first(i + 1, (i + 1) % 2)
+                middle(i, i % 2)
+                if i > 0:
+                    final(i - 1, (i - 1) % 2)
+            final(pairs - 1, (pairs - 1) % 2)
+            return
 
         @pl.loop(0, pairs // 2)
         def _(h):
@@ -283,7 +294,7 @@
             def mix(i, b):
                 att[p, :, lanes(i)] = unstack(dot_nn(pbuf[b][:, :keys], qkv[:keys, lanes(i, 2 * D)])).astype(BF)
 
-            pair_pipeline(scores, softmax, mix)
+            pair_pipeline(keys == seq, scores, softmax, mix)
 
         by_piece(p, attend)
         put(1, p, att.at[p], a_o).start()
@@ -411,8 +422,7 @@
         for idx in range(3, 6):
             arrived(idx)
         back_down(2)
-        acc[...] += back_up(1)
-        acc[...] += back_up(2)
+        acc[...] += back_up(1) + back_up(2)
         for idx in range(3, 6):
             fetch_next(idx)
         for idx in range(6, 8):
@@ -457,6 +467,12 @@
                     dkvt[lanes(i, D), :keys] += dv
 
             slopes(0, 0)
+            if keys == seq:
+                for i in range(pairs):
+                    if i + 1 < pairs:
+                        slopes(i + 1, (i + 1) % 2)
+                    grads(i, i % 2)
+                return
 
             @pl.loop(0, pairs // 2)
             def _(h):

time: 335 us -> 328 us (0.979)
  Pallas kernels: 334 us -> 327 us
    pallas_call x1, Pallas kernels: 301 us -> 294 us  [run_pipeline(): pl.pallas_call(functools.partial(pipeline_kernel, stages, seq, width), ou...]
where the time goes in v6:
time: 328 us
  Pallas kernels  327 us (100%)
    pallas_call x1, Pallas kernels, run_pipeline(): pl.pallas_call(functools.partial(pipeline_kernel, stages, seq, width), ou...  294 us
    pallas_call x1, Pallas kernels, weight_grads(): pl.pallas_call(wgrad_kernel, out_shape=[jax.ShapeDtypeStruct((1,) + sh, F...  33.4 us

profile of v6, /device:TPU:0, one launch (start us, length us, event | category | flops | bytes accessed | tf_op | source)
XLA Modules:
  0.0 328.2 jit_solution(13392119993362664967)
XLA Ops:
  0.6 293.9 %pipeline.1 = (f32[8,128]{1,0:T(8,128)}, f32[2,1280]{1,0:T(2,128)}, bf16[512,1280]{1,0:T(8,128)(2,1)}, bf16[512,1280]{1,0:T(8,128)(2,1)}, bf16[512,1280]{1,0:T(8...) custom-call(bf16[1,512,1280]{2,1,0:T(8,128)(2,1)} %x_ref.1, ...), custom_call_target="tpu_custom_call" | custom-call | tf_op jit(solution)/shard_map/pipeline/pallas_call | solution.py:565
  294.6 33.4 %weight_grads.1 = (f32[1,1280,3840]{2,1,0:T(8,128)}, f32[1,1280,1280]{2,1,0:T(8,128)}, f32[1,1280,5120]{2,1,0:T(8,128)}, f32[1,5120,1280]{2,1,0:T(8,128)}, f32[1,2,1280]{2,1,0:T(2,128)}, /*index=5*/f32[1,128]{1,0:T(1,128)}) custom-call(bf16[512,1280]{1,0:T(8,128)(2,1)} %get-tuple-element.22.n1, bf16[512,3840]{1,0:T(8,128)(2,1)} %get-tuple-element.23.dqkv, ...), custom_call_target="tpu_custom_call" | custom-call | tf_op jit(solution)/shard_map/weight_grads/pallas_call | solution.py:644
